TPU v7x, 32 devices: a whole 2x2x4 slice. The times are simulated.
32 devices in a mesh: gx: 4 (over z), gy: 4 (over y, x), gz: 2 (over core).
Axes of the slice: x: 2, y: 2, z: 4, core: 2. Of those that a mesh axis runs over, the one named last changes fastest.
Arguments:
- cotangent: float32 [19, 32, 64, 256], P(None, 'gx', 'gy', 'gz'), may hold values from -6 to 6
- densities: float32 [3, 32, 64, 256], P(None, 'gx', 'gy', 'gz'), may hold values from 0.3 to 2.2
- velocities: float32 [3, 3, 32, 64, 256], P(None, None, 'gx', 'gy', 'gz'), may hold values from -0.16 to 0.16
- adhesion: float32 [32, 64, 256], P('gx', 'gy', 'gz'), may hold values from -1 to 1
- fluid: int32 [32, 64, 256], P('gx', 'gy', 'gz'), may hold values 0 or 1
Outputs:
- initial_cotangent: float32 [19, 32, 64, 256], P(None, 'gx', 'gy', 'gz')
- adhesion_grad: float32 [32, 64, 256], P('gx', 'gy', 'gz')
All inputs are finite; a program needn't handle non-finite values. No bound on the sum of `fluid` on one device may be relied on, other than what follows from the above.
Results may differ from a plain program's by a relative error of at most 0.00002.
Values sent between devices are 32-bit elements; how exact they have to be, the bound alone decides.
No kernel may reach another device: no remote copies, remote signals or barrier semaphores. Data moves between devices by JAX's collectives and lax.ppermute only.
A program may use at most 64 MiB of HBM per device.

v0:
```python
import functools

import jax
import jax.numpy as jnp
from jax import lax
from jax.experimental import pallas as pl
from jax.experimental.pallas import tpu as pltpu
from jax.sharding import PartitionSpec as P

DIRECTIONS = (
    (0, 0, 0),
    (1, 0, 0),
    (-1, 0, 0),
    (0, 1, 0),
    (0, -1, 0),
    (0, 0, 1),
    (0, 0, -1),
    (1, 1, 0),
    (-1, -1, 0),
    (1, -1, 0),
    (-1, 1, 0),
    (1, 0, 1),
    (-1, 0, -1),
    (1, 0, -1),
    (-1, 0, 1),
    (0, 1, 1),
    (0, -1, -1),
    (0, 1, -1),
    (0, -1, 1),
)
OPPOSITE = (0, 2, 1, 4, 3, 6, 5, 8, 7, 10, 9, 12, 11, 14, 13, 16, 15, 18, 17)
RELAX_TIME = 0.8
COUPLING = -5.0
W_REST = 1.0 / 3.0 / RELAX_TIME
W_AXIS = 1.0 / 18.0 / RELAX_TIME
W_DIAG = 1.0 / 36.0 / RELAX_TIME
C18 = 1.0 / 18.0
C36 = 1.0 / 36.0

XP = tuple(i for i in range(19) if DIRECTIONS[i][0] == 1)
XM = tuple(i for i in range(19) if DIRECTIONS[i][0] == -1)
YP = tuple(i for i in range(19) if DIRECTIONS[i][1] == 1)
YM = tuple(i for i in range(19) if DIRECTIONS[i][1] == -1)
EDGE = {(1, 1): 7, (-1, -1): 8, (1, -1): 9, (-1, 1): 10}
PAD = 8
VMEM_LIMIT = 24 * 1024 * 1024
X_AXES = ("gx", "gz")


class Plan:
    def __init__(self, n_gx, n_gy, n_gz, block, steps):
        self.tiles = n_gz
        self.nx = block[0] // n_gz
        self.ny = block[1]
        self.lanes = block[2]
        self.steps = steps
        self.chain_x = n_gx * n_gz
        self.chain_y = n_gy
        self.n_gz = n_gz
        self.q_rho = 19
        self.q_vel = 19 + steps
        self.q_adh = 19 + 4 * steps
        self.q_fl = self.q_adh + 1
        self.nq = self.q_fl + 1
        self.n_state = steps + 2
        self.s_adh = steps
        self.s_fl = steps + 1
        self.rows = self.ny + 2 * PAD

    def padded(self, count):
        return (count, self.tiles, self.nx + 2, self.rows, self.lanes)

    def x_layout(self, last):
        at = 0 if last else 5 * self.ny
        out = {}
        if not last:
            out["own"] = at
            at += self.ny
        out["beyond"] = at
        at += self.ny
        out["ends"] = at
        out["rows"] = at + 8
        return out

    def y_layout(self, last):
        at = 0
        out = {}
        if not last:
            out["edges"] = 5 * self.nx
            at = 5 * self.nx + 2
            out["own"] = at
            at += self.nx + 2
        out["beyond"] = at
        at += self.nx + 2
        out["rows"] = -(-at // 8) * 8
        return out

    def input_y_layout(self):
        pops = self.n_state * (self.nx + 2)
        edges = pops + 5 * self.nx
        return {"pops": pops, "edges": edges, "rows": -(-(edges + 2) // 8) * 8}


def flag(cond, shape):
    return jnp.full(shape, cond.astype(jnp.int32), jnp.int32) == 1


def chain_place(axes, count):
    if axes == "gy":
        place = lax.axis_index("gy")
    else:
        place = lax.axis_index("gx") * lax.axis_size("gz") + lax.axis_index("gz")
    return place % 2 == 0, place < count - 1, place > 0


def pick(cond, one, other):
    return jnp.where(flag(cond, one.shape), one, other)


def halo_pair(place, first, second):
    even, has_plus, has_minus = place
    zero = jnp.zeros_like(first)
    plus = pick(has_plus, pick(even, first, second), zero)
    minus = pick(has_minus, pick(even, second, first), zero)
    return plus, minus


def z_shift(tiles, by):
    lanes = tiles[0].shape[-1]
    lane = lax.broadcasted_iota(jnp.int32, tiles[0].shape, len(tiles[0].shape) - 1)
    count = len(tiles)
    axis = len(tiles[0].shape) - 1
    if by == 1:
        rolled = [pltpu.roll(v, lanes - 1, axis) for v in tiles] + [jnp.zeros_like(tiles[0])]
        return [jnp.where(lane == lanes - 1, rolled[t + 1], rolled[t]) for t in range(count)]
    rolled = [jnp.zeros_like(tiles[0])] + [pltpu.roll(v, 1, axis) for v in tiles]
    return [jnp.where(lane == 0, rolled[t], rolled[t + 1]) for t in range(count)]


def each(fn, *lists):
    return [fn(*items) for items in zip(*lists)]


def split_kernel(plan, cot, dens, vel, adh, fluid, *rest):
    n = plan.n_gz
    outs = rest[:n]
    whole, sems = rest[n], rest[n + 1]
    me = lax.axis_index("gz")
    nx = plan.nx
    copies = []
    for k, d in enumerate(list(range(1, n)) + [0]):
        chunk = pl.ds(lax.rem(me + d, n) * nx, nx)
        out = outs[d]
        pairs = [
            (cot.at[:, chunk], out.at[0:19]),
            (dens.at[:, chunk], out.at[plan.q_rho : plan.q_rho + plan.steps]),
            (adh.at[chunk], out.at[plan.q_adh]),
            (fluid.at[chunk], whole.at[d]),
        ]
        for s in range(plan.steps):
            at = plan.q_vel + 3 * s
            pairs.append((vel.at[s, :, chunk], out.at[at : at + 3]))
        for j, (src, dst) in enumerate(pairs):
            copies.append(pltpu.make_async_copy(src, dst, sems.at[k, j]))
    for copy in copies:
        copy.start()
    for copy in copies:
        copy.wait()
    for d in range(n):
        outs[d][plan.q_fl] = whole[d].astype(jnp.float32)


def tile_of(plan, refs, t, index):
    me = lax.axis_index("gz")
    out = refs[0][index]
    for d in range(1, plan.n_gz):
        out = pick(lax.rem(me - t + plan.n_gz, plan.n_gz) == d, refs[d][index], out)
    return out


def state_index(plan, k):
    if k < plan.steps:
        return plan.q_rho + k
    return plan.q_adh if k == plan.s_adh else plan.q_fl


def input_x_kernel(plan, *refs):
    n = plan.n_gz
    parts, (out_a, out_b) = refs[:n], refs[n:]
    even = chain_place(X_AXES, plan.chain_x)[0]
    for t in range(plan.tiles):
        for j in range(5 + plan.n_state):
            up = XM[j] if j < 5 else state_index(plan, j - 5)
            down = XP[j] if j < 5 else state_index(plan, j - 5)
            plus = tile_of(plan, parts, t, (up, plan.nx - 1))
            minus = tile_of(plan, parts, t, (down, 0))
            out_a[j, t] = pick(even, plus, minus)
            out_b[j, t] = pick(even, minus, plus)


def input_y_kernel(plan, *refs):
    n = plan.n_gz
    parts = refs[:n]
    xr_a, xr_b, out_a, out_b, up, down = refs[n:]
    nx, ny = plan.nx, plan.ny
    lay = plan.input_y_layout()
    place_x = chain_place(X_AXES, plan.chain_x)
    even = chain_place("gy", plan.chain_y)[0]
    up[...] = jnp.zeros_like(up)
    down[...] = jnp.zeros_like(down)
    top = slice(ny - 1, ny)
    low = slice(0, 1)
    for t in range(plan.tiles):
        for k in range(plan.n_state):
            base = k * (nx + 2)
            plus, minus = halo_pair(place_x, xr_a[5 + k, t], xr_b[5 + k, t])
            for x in range(-1, nx + 1):
                if x < 0:
                    plane = minus
                elif x == nx:
                    plane = plus
                else:
                    plane = tile_of(plan, parts, t, (state_index(plan, k), x))
                r = base + x + 1
                up[t, r : r + 1] = plane[top]
                down[t, r : r + 1] = plane[low]
        for j in range(5):
            for x in range(nx):
                r = lay["pops"] + j * nx + x
                up[t, r : r + 1] = tile_of(plan, parts, t, (YM[j], x, top))
                down[t, r : r + 1] = tile_of(plan, parts, t, (YP[j], x, low))
        r = lay["edges"]
        for side, out, rows in ((-1, up, top), (1, down, low)):
            j = XM.index(EDGE[(-1, side)])
            out[t, r : r + 1] = halo_pair(place_x, xr_a[j, t], xr_b[j, t])[1][rows]
            j = XP.index(EDGE[(1, side)])
            out[t, r + 1 : r + 2] = halo_pair(place_x, xr_a[j, t], xr_b[j, t])[0][rows]
        out_a[t] = pick(even, up[t], down[t])
        out_b[t] = pick(even, down[t], up[t])


def fill_inputs(plan, parts, xr_a, xr_b, yr_a, yr_b, state, apad):
    nx, ny = plan.nx, plan.ny
    lay = plan.input_y_layout()
    place_x = chain_place(X_AXES, plan.chain_x)
    place_y = chain_place("gy", plan.chain_y)
    own = slice(PAD, PAD + ny)
    first, last = slice(PAD - 1, PAD), slice(PAD + ny, PAD + ny + 1)
    for t in range(plan.tiles):
        y_plus, y_minus = halo_pair(place_y, yr_a[t], yr_b[t])
        for k in range(plan.n_state):
            plus, minus = halo_pair(place_x, xr_a[5 + k, t], xr_b[5 + k, t])
            for x in range(-1, nx + 1):
                if x < 0:
                    plane = minus
                elif x == nx:
                    plane = plus
                else:
                    plane = tile_of(plan, parts, t, (state_index(plan, k), x))
                r = k * (nx + 2) + x + 1
                state[k, t, x + 1, own] = plane
                state[k, t, x + 1, first] = y_minus[r : r + 1]
                state[k, t, x + 1, last] = y_plus[r : r + 1]
        fl = plan.s_fl
        for x in range(nx):
            mask = state[fl, t, x + 1, own]
            for i in range(19):
                apad[i, t, x + 1, own] = mask * tile_of(plan, parts, t, (i, x))
            mask_first = state[fl, t, x + 1, first]
            mask_last = state[fl, t, x + 1, last]
            for j in range(5):
                r = lay["pops"] + j * nx + x
                apad[YP[j], t, x + 1, last] = mask_last * y_plus[r : r + 1]
                apad[YM[j], t, x + 1, first] = mask_first * y_minus[r : r + 1]
        for j in range(5):
            plus, minus = halo_pair(place_x, xr_a[j, t], xr_b[j, t])
            apad[XP[j], t, nx + 1, own] = state[fl, t, nx + 1, own] * plus
            apad[XM[j], t, 0, own] = state[fl, t, 0, own] * minus
        r = lay["edges"]
        for side, rows, msg in ((1, last, y_plus), (-1, first, y_minus)):
            apad[EDGE[(-1, side)], t, 0, rows] = state[fl, t, 0, rows] * msg[r : r + 1]
            apad[EDGE[(1, side)], t, nx + 1, rows] = state[fl, t, nx + 1, rows] * msg[r + 1 : r + 2]


def complete_back(plan, last_phase, ksum, yr_a, yr_b, total):
    nx, ny = plan.nx, plan.ny
    lay = plan.y_layout(last_phase)
    place_y = chain_place("gy", plan.chain_y)
    total[...] = ksum[...]
    for t in range(plan.tiles):
        plus, minus = halo_pair(place_y, yr_a[t], yr_b[t])
        for x in range(nx + 2):
            r = lay["beyond"] + x
            rows = slice(PAD + ny - 1, PAD + ny)
            total[t, x, rows] = total[t, x, rows] + plus[r : r + 1]
            rows = slice(PAD, PAD + 1)
            total[t, x, rows] = total[t, x, rows] + minus[r : r + 1]
            if not last_phase:
                r = lay["own"] + x
                rows = slice(PAD + ny, PAD + ny + 1)
                total[t, x, rows] = total[t, x, rows] + plus[r : r + 1]
                rows = slice(PAD - 1, PAD)
                total[t, x, rows] = total[t, x, rows] + minus[r : r + 1]


def fill_next(plan, s, state, a_in, ksum, xr_a, xr_b, yr_a, yr_b, grad_in, grad_out, total, apad):
    nx, ny = plan.nx, plan.ny
    lay = plan.y_layout(False)
    place_x = chain_place(X_AXES, plan.chain_x)
    place_y = chain_place("gy", plan.chain_y)
    own = slice(PAD, PAD + ny)
    first, last = slice(PAD - 1, PAD), slice(PAD + ny, PAD + ny + 1)
    complete_back(plan, False, ksum, yr_a, yr_b, total)

    def extra(t, x, rows):
        mask = state[plan.s_fl, t, x + 1, rows]
        rho = state[s + 1, t, x + 1, rows]
        return (-COUPLING) * mask * jnp.exp(-rho) * total[t, x + 1, rows]

    for t in range(plan.tiles):
        y_plus, y_minus = halo_pair(place_y, yr_a[t], yr_b[t])
        for x in range(nx):
            more = extra(t, x, own)
            part = (1.0 - state[plan.s_fl, t, x + 1, own]) * total[t, x + 1, own]
            grad_out[t, x] = -part if grad_in is None else grad_in[t, x] - part
            for i in range(19):
                apad[i, t, x + 1, own] = a_in[i, t, x] + more
            more_first, more_last = extra(t, x, first), extra(t, x, last)
            for j in range(5):
                r = j * nx + x
                apad[YP[j], t, x + 1, last] = y_plus[r : r + 1] + more_last
                apad[YM[j], t, x + 1, first] = y_minus[r : r + 1] + more_first
        more_plus, more_minus = extra(t, nx, own), extra(t, -1, own)
        for j in range(5):
            rows = slice(j * ny, (j + 1) * ny)
            plus, minus = halo_pair(place_x, xr_a[t, rows], xr_b[t, rows])
            apad[XP[j], t, nx + 1, own] = plus + more_plus
            apad[XM[j], t, 0, own] = minus + more_minus
        r = lay["edges"]
        for side, rows, msg in ((1, last, y_plus), (-1, first, y_minus)):
            apad[EDGE[(-1, side)], t, 0, rows] = msg[r : r + 1] + extra(t, -1, rows)
            apad[EDGE[(1, side)], t, nx + 1, rows] = msg[r + 1 : r + 2] + extra(t, nx, rows)


def fill_phi(plan, s, state, phi):
    for t in range(plan.tiles):
        for x in range(plan.nx + 2):
            mask = state[plan.s_fl, t, x]
            psi = 1.0 - jnp.exp(-state[s, t, x])
            phi[t, x] = COUPLING * mask * psi + (1.0 - mask) * state[plan.s_adh, t, x]


def force_at(plan, phi, x, rows):
    tiles = range(plan.tiles)

    def at(dx, dy):
        return [phi[t, x + 1 + dx, rows.start + dy : rows.stop + dy] for t in tiles]

    sub, add = (lambda a, b: a - b), (lambda a, b: a + b)
    xp, xm, yp, ym, mid = at(1, 0), at(-1, 0), at(0, 1), at(0, -1), at(0, 0)
    pp, pm, mp, mm = at(1, 1), at(1, -1), at(-1, 1), at(-1, -1)
    dx, dy = each(sub, xp, xm), each(sub, yp, ym)
    zd = each(lambda m, a, b, c, d: C18 * m + C36 * ((a + b) + (c + d)), mid, xp, xm, yp, ym)
    dxu, dxd, dyu, dyd = z_shift(dx, 1), z_shift(dx, -1), z_shift(dy, 1), z_shift(dy, -1)
    px = each(
        lambda d, u, w, a, b, c, e: C18 * d + C36 * ((u + w) + ((a - c) + (b - e))),
        dx, dxu, dxd, pp, pm, mp, mm,
    )
    py = each(
        lambda d, u, w, a, b, c, e: C18 * d + C36 * ((u + w) + ((a - b) + (c - e))),
        dy, dyu, dyd, pp, pm, mp, mm,
    )
    pz = each(sub, z_shift(zd, 1), z_shift(zd, -1))
    return px, py, pz


def cells(plan, s, state, solid, fresh, vel, phi, apad, a_out, vpad, kept):
    nx, ny = plan.nx, plan.ny
    tiles = range(plan.tiles)
    for x in range(nx):
        for r0 in range(0, ny, 8):
            own = slice(PAD + r0, PAD + r0 + 8)
            here = slice(r0, r0 + 8)
            b = [[apad[0, t, x + 1, own] for t in tiles]]
            for i in range(1, 19):
                cx, cy, cz = DIRECTIONS[i]
                rows = slice(own.start + cy, own.stop + cy)
                came = [apad[i, t, x + 1 + cx, rows] for t in tiles]
                if cz:
                    came = z_shift(came, cz)
                if fresh:
                    open_to = [state[plan.s_fl, t, x + 1 + cx, rows] for t in tiles]
                    if cz:
                        open_to = z_shift(open_to, cz)
                    wall = [1.0 - v for v in open_to]
                    for t in tiles:
                        solid[i - 1, t, x, here] = wall[t]
                else:
                    wall = [solid[i - 1, t, x, here] for t in tiles]
                back = [apad[OPPOSITE[i], t, x + 1, own] for t in tiles]
                b.append(each(lambda c, w, o: c + w * o, came, wall, back))
            force = force_at(plan, phi, x, own)
            for t in tiles:
                g = [v[t] for v in b]
                sm = {i: g[i] + g[i + 1] for i in range(1, 19, 2)}
                df = {i: g[i] - g[i + 1] for i in range(1, 19, 2)}
                sxy, sxz, syz = sm[7] + sm[9], sm[11] + sm[13], sm[15] + sm[17]
                ux, uy, uz = vel(t, 0, x, here), vel(t, 1, x, here), vel(t, 2, x, here)
                m1x = W_AXIS * df[1] + W_DIAG * ((df[7] + df[9]) + (df[11] + df[13]))
                m1y = W_AXIS * df[3] + W_DIAG * ((df[7] - df[9]) + (df[15] + df[17]))
                m1z = W_AXIS * df[5] + W_DIAG * ((df[11] - df[13]) + (df[15] - df[17]))
                mxx = W_AXIS * sm[1] + W_DIAG * (sxy + sxz)
                myy = W_AXIS * sm[3] + W_DIAG * (sxy + syz)
                mzz = W_AXIS * sm[5] + W_DIAG * (sxz + syz)
                mxy = W_DIAG * (sm[7] - sm[9])
                mxz = W_DIAG * (sm[11] - sm[13])
                myz = W_DIAG * (sm[15] - sm[17])
                m0 = W_REST * g[0] + W_AXIS * ((sm[1] + sm[3]) + sm[5]) + W_DIAG * ((sxy + sxz) + syz)
                vx = mxx * ux + mxy * uy + mxz * uz
                vy = mxy * ux + myy * uy + myz * uz
                vz = mxz * ux + myz * uy + mzz * uz
                mbx = 3.0 * (m1x - ux * m0) + 9.0 * vx
                mby = 3.0 * (m1y - uy * m0) + 9.0 * vy
                mbz = 3.0 * (m1z - uz * m0) + 9.0 * vz
                usq = ux * ux + uy * uy + uz * uz
                rhobar = m0 * (1.0 + 1.5 * usq) - 4.5 * (ux * vx + uy * vy + uz * vz)
                fade = jnp.exp(-state[s, t, x + 1, own])
                mask = state[plan.s_fl, t, x + 1, own]
                pull = mbx * force[0][t] + mby * force[1][t] + mbz * force[2][t]
                rhobar = rhobar - RELAX_TIME * pull * fade
                scale = RELAX_TIME * mask * (1.0 - fade)
                vpad[0, t, x, own] = scale * mbx
                vpad[1, t, x, own] = scale * mby
                vpad[2, t, x, own] = scale * mbz
                rb, mx, my, mz = mask * rhobar, mask * mbx, mask * mby, mask * mbz
                damp = (1.0 - 1.0 / RELAX_TIME) * mask
                a_out(0, t, x, here, rb + damp * g[0])
                for i in range(1, 19, 2):
                    cx, cy, cz = DIRECTIONS[i]
                    along = None
                    for c, m in ((cx, mx), (cy, my), (cz, mz)):
                        if c == 1:
                            along = m if along is None else along + m
                        elif c == -1:
                            along = along - m
                    a_out(i, t, x, here, (rb + along) + damp * g[i])
                    a_out(i + 1, t, x, here, (rb - along) + damp * g[i + 1])


def sums_of_back(plan, vpad, kext):
    nx, ny = plan.nx, plan.ny
    tiles = range(plan.tiles)
    add = lambda a, b: a + b
    chunks = [slice(PAD + r, PAD + r + 8) for r in range(0, ny, 8)]
    chunks += [slice(PAD - 1, PAD), slice(PAD + ny, PAD + ny + 1)]
    for x in range(-1, nx + 1):
        for rows in chunks:

            def at(k, dx, dy):
                if not 0 <= x + dx < nx:
                    return None
                return [vpad[k, t, x + dx, rows.start + dy : rows.stop + dy] for t in tiles]

            def combine(a, b, sign):
                if a is None and b is None:
                    return None
                if b is None:
                    return a
                if a is None:
                    return b if sign > 0 else [-v for v in b]
                return each((lambda p, q: p + q) if sign > 0 else (lambda p, q: p - q), a, b)

            def times(c, a):
                return None if a is None else [c * v for v in a]

            dx0 = combine(at(0, 1, 0), at(0, -1, 0), -1)
            dxs = combine(
                combine(at(0, 1, 1), at(0, -1, 1), -1), combine(at(0, 1, -1), at(0, -1, -1), -1), 1
            )
            dy0 = combine(at(1, 0, 1), at(1, 0, -1), -1)
            dys = combine(
                combine(at(1, 1, 1), at(1, 1, -1), -1), combine(at(1, -1, 1), at(1, -1, -1), -1), 1
            )
            zsum = times(C36, combine(dx0, dy0, 1))
            side = combine(combine(at(2, 1, 0), at(2, -1, 0), 1), combine(at(2, 0, 1), at(2, 0, -1), 1), 1)
            zdif = combine(times(C18, at(2, 0, 0)), times(C36, side), 1)
            flat = combine(times(C18, combine(dx0, dy0, 1)), times(C36, combine(dxs, dys, 1)), 1)
            up = z_shift(combine(zsum, zdif, 1), 1)
            down = z_shift(combine(zsum, zdif, -1), -1)
            for t in tiles:
                kext[t, x + 1, rows] = -(flat[t] + (up[t] + down[t]))


def pack_x(plan, last_phase, a_of, kext, out_a, out_b):
    nx, ny = plan.nx, plan.ny
    lay = plan.x_layout(last_phase)
    even = chain_place(X_AXES, plan.chain_x)[0]
    own = slice(PAD, PAD + ny)

    def put(t, rows, plus, minus):
        out_a[t, rows] = pick(even, plus, minus)
        out_b[t, rows] = pick(even, minus, plus)

    for t in range(plan.tiles):
        if not last_phase:
            for j in range(5):
                put(t, slice(j * ny, (j + 1) * ny), a_of(XM[j], t, nx - 1), a_of(XP[j], t, 0))
            put(t, slice(lay["own"], lay["own"] + ny), kext[t, nx, own], kext[t, 1, own])
        put(t, slice(lay["beyond"], lay["beyond"] + ny), kext[t, nx + 1, own], kext[t, 0, own])
        r = lay["ends"]
        blank = jnp.zeros((8, plan.lanes), jnp.float32)
        out_a[t, r : r + 8] = blank
        out_b[t, r : r + 8] = blank
        for j, row in enumerate((PAD - 1, PAD + ny)):
            rows = slice(row, row + 1)
            put(t, slice(r + j, r + j + 1), kext[t, nx + 1, rows], kext[t, 0, rows])
            if not last_phase:
                put(t, slice(r + 2 + j, r + 3 + j), kext[t, nx, rows], kext[t, 1, rows])


def pack_rows(plan, a_of_row, up, down):
    for t in range(plan.tiles):
        up[t] = jnp.zeros_like(up[t])
        down[t] = jnp.zeros_like(down[t])
        for j in range(5):
            for x in range(plan.nx):
                r = j * plan.nx + x
                up[t, r : r + 1] = a_of_row(YM[j], t, x, plan.ny - 1)
                down[t, r : r + 1] = a_of_row(YP[j], t, x, 0)


def finish_step(plan, last_phase, a_ref, vpad, kext, out_a, out_b, up, down):
    sums_of_back(plan, vpad, kext)
    pack_x(plan, last_phase, lambda i, t, x: a_ref[i, t, x], kext, out_a, out_b)
    if not last_phase:
        pack_rows(plan, lambda i, t, x, row: a_ref[i, t, x, row : row + 1], up, down)


def blank_rows(plan, ref):
    blank = jnp.zeros((PAD, plan.lanes), jnp.float32)
    for k in range(3):
        for t in range(plan.tiles):
            for x in range(plan.nx):
                ref[k, t, x, 0:PAD] = blank
                ref[k, t, x, PAD + plan.ny :] = blank


def first_kernel(plan, *refs):
    n = plan.n_gz
    parts = refs[:n]
    xr_a, xr_b, yr_a, yr_b = refs[n : n + 4]
    state, solid, vels, a_ref, kext, out_a, out_b, up, down, apad, phi, vpad = refs[n + 4 :]
    s = plan.steps - 1
    last_phase = s == 0
    fill_inputs(plan, parts, xr_a, xr_b, yr_a, yr_b, state, apad)
    for t in range(plan.tiles):
        for k in range(3 * (plan.steps - 1)):
            vels[k, t] = tile_of(plan, parts, t, (plan.q_vel + k,))
    fill_phi(plan, s, state, phi)
    blank_rows(plan, vpad)

    def vel(t, k, x, here):
        return tile_of(plan, parts, t, (plan.q_vel + 3 * s + k, x, here))

    def a_out(i, t, x, here, value):
        a_ref[i, t, x, here] = value

    cells(plan, s, state, solid, True, vel, phi, apad, a_out, vpad, None)
    finish_step(plan, last_phase, a_ref, vpad, kext, out_a, out_b, up, down)


def next_kernel(plan, s, has_grad, *refs):
    refs = list(refs)
    take = lambda k: [refs.pop(0) for _ in range(k)]
    last_phase = s == 0
    state, solid, vels, a_in, ksum, xr_a, xr_b, yr_a, yr_b = take(9)
    grad_in = take(1)[0] if has_grad else None
    if last_phase:
        tiles_out = take(plan.n_gz)
        kext, out_a, out_b, grad_out, apad, phi, vpad, total, a_ref = take(9)
        up = down = None
    else:
        a_ref, kext, out_a, out_b, up, down, grad_out, apad, phi, vpad, total = take(11)
    fill_next(plan, s, state, a_in, ksum, xr_a, xr_b, yr_a, yr_b, grad_in, grad_out, total, apad)
    fill_phi(plan, s, state, phi)
    blank_rows(plan, vpad)

    def vel(t, k, x, here):
        return vels[3 * s + k, t, x, here]

    def a_out(i, t, x, here, value):
        if last_phase:
            a_ref[t, i, x, here] = value
        else:
            a_ref[i, t, x, here] = value

    cells(plan, s, state, solid, False, vel, phi, apad, a_out, vpad, None)
    finish_step(plan, last_phase, a_ref, vpad, kext, out_a, out_b, up, down)
    if last_phase:
        me = lax.axis_index("gz")
        for d in range(plan.n_gz):
            tiles_out[d][...] = a_ref[lax.rem(me + d, plan.n_gz)]


def y_kernel(plan, last_phase, *refs):
    if last_phase:
        kext, xr_a, xr_b, ksum, out_a, out_b, up, down = refs
        up[...] = jnp.zeros_like(up)
        down[...] = jnp.zeros_like(down)
    else:
        kext, xr_a, xr_b, up_in, down_in, ksum, out_a, out_b, up, down = refs
        up[...] = up_in[...]
        down[...] = down_in[...]
    nx, ny = plan.nx, plan.ny
    lay_x, lay_y = plan.x_layout(last_phase), plan.y_layout(last_phase)
    place_x = chain_place(X_AXES, plan.chain_x)
    even = chain_place("gy", plan.chain_y)[0]
    own = slice(PAD, PAD + ny)
    ksum[...] = kext[...]
    for t in range(plan.tiles):

        def add(x, rows, msg_rows, side):
            part = halo_pair(place_x, xr_a[t, msg_rows], xr_b[t, msg_rows])[side]
            ksum[t, x + 1, rows] = ksum[t, x + 1, rows] + part

        for x, side in ((nx - 1, 0), (0, 1)):
            add(x, own, slice(lay_x["beyond"], lay_x["beyond"] + ny), side)
            for j, row in enumerate((PAD - 1, PAD + ny)):
                r = lay_x["ends"] + j
                add(x, slice(row, row + 1), slice(r, r + 1), side)
        if not last_phase:
            for x, side in ((nx, 0), (-1, 1)):
                add(x, own, slice(lay_x["own"], lay_x["own"] + ny), side)
                for j, row in enumerate((PAD - 1, PAD + ny)):
                    r = lay_x["ends"] + 2 + j
                    add(x, slice(row, row + 1), slice(r, r + 1), side)
            r = lay_y["edges"]
            for side, out, row in ((-1, up, ny - 1), (1, down, 0)):
                j = XM.index(EDGE[(-1, side)]) * ny + row
                out[t, r : r + 1] = halo_pair(place_x, xr_a[t, j : j + 1], xr_b[t, j : j + 1])[1]
                j = XP.index(EDGE[(1, side)]) * ny + row
                out[t, r + 1 : r + 2] = halo_pair(place_x, xr_a[t, j : j + 1], xr_b[t, j : j + 1])[0]
        for x in range(nx + 2):
            r = lay_y["beyond"] + x
            up[t, r : r + 1] = ksum[t, x, PAD + ny : PAD + ny + 1]
            down[t, r : r + 1] = ksum[t, x, PAD - 1 : PAD]
            if not last_phase:
                r = lay_y["own"] + x
                up[t, r : r + 1] = ksum[t, x, PAD + ny - 1 : PAD + ny]
                down[t, r : r + 1] = ksum[t, x, PAD : PAD + 1]
        out_a[t] = pick(even, up[t], down[t])
        out_b[t] = pick(even, down[t], up[t])


def close_kernel(plan, state, ksum, yr_a, yr_b, grad_in, *rest):
    n = plan.n_gz
    outs, (total, both) = rest[:n], rest[n:]
    own = slice(PAD, PAD + plan.ny)
    complete_back(plan, True, ksum, yr_a, yr_b, total)
    for t in range(plan.tiles):
        for x in range(plan.nx):
            mask = state[plan.s_fl, t, x + 1, own]
            rho = state[0, t, x + 1, own]
            back = total[t, x + 1, own]
            both[t, 0, x] = (-COUPLING) * mask * jnp.exp(-rho) * back
            both[t, 1, x] = grad_in[t, x] - (1.0 - mask) * back
    me = lax.axis_index("gz")
    for d in range(n):
        outs[d][...] = both[lax.rem(me + d, n)]


def join_kernel(plan, *refs):
    n = plan.n_gz
    a_parts, r_parts, (out, grad) = refs[:n], refs[n : 2 * n], refs[2 * n :]
    me = lax.axis_index("gz")
    for d in range(n):
        chunk = pl.ds(lax.rem(me - d + n, n) * plan.nx, plan.nx)
        for i in range(19):
            out[i, chunk] = a_parts[d][i] + r_parts[d][0]
        grad[chunk] = r_parts[d][1]


def swaps(count):
    one = [(i, i ^ 1) for i in range(count)]
    two = [(i, (i + 1) % count if i % 2 else (i - 1) % count) for i in range(count)]
    return one, two


def swap_along(axes, count, first, second):
    one, two = swaps(count)
    return lax.ppermute(first, axes, one), lax.ppermute(second, axes, two)


def call(kernel, name, outs, scratch, args, flops, in_hbm=False):
    spec = pl.BlockSpec(memory_space=pl.ANY if in_hbm else pltpu.VMEM)
    return pl.pallas_call(
        kernel,
        name=name,
        out_shape=tuple(jax.ShapeDtypeStruct(shape, jnp.float32) for shape in outs),
        in_specs=[spec] * len(args),
        out_specs=tuple(pl.BlockSpec(memory_space=pltpu.VMEM) for _ in outs),
        scratch_shapes=scratch,
        cost_estimate=pl.CostEstimate(flops=flops, bytes_accessed=0, transcendentals=0),
        compiler_params=pltpu.CompilerParams(vmem_limit_bytes=VMEM_LIMIT),
    )(*args)


def per_device(cotangent, densities, velocities, adhesion, fluid):
    n = lax.axis_size("gz")
    plan = Plan(lax.axis_size("gx"), lax.axis_size("gy"), n, adhesion.shape, densities.shape[0])
    tiles, nx, ny, lanes, steps = plan.tiles, plan.nx, plan.ny, plan.lanes, plan.steps
    f32 = jnp.float32
    field = (tiles, nx, ny, lanes)
    padded = plan.padded(1)[1:]

    def along_x(first, second):
        return swap_along(X_AXES, plan.chain_x, first, second)

    def along_y(first, second):
        return swap_along("gy", plan.chain_y, first, second)

    def within_gz(parts):
        return [parts[0]] + [
            lax.ppermute(parts[d], "gz", [(i, (i + d) % n) for i in range(n)]) for d in range(1, n)
        ]

    part = (plan.nq, nx, ny, lanes)
    parts = call(
        functools.partial(split_kernel, plan),
        "split",
        [part] * n,
        [pltpu.VMEM((n, nx, ny, lanes), jnp.int32), pltpu.SemaphoreType.DMA((n, 4 + steps))],
        (cotangent, densities, velocities, adhesion, fluid),
        1000,
        in_hbm=True,
    )
    parts = within_gz(parts)

    msg = (5 + plan.n_state, tiles, ny, lanes)
    xr = along_x(*call(functools.partial(input_x_kernel, plan), "input_x", [msg] * 2, [], parts, 1000))
    msg = (tiles, plan.input_y_layout()["rows"], lanes)
    buffers = [pltpu.VMEM(msg, f32)] * 2
    yr = along_y(
        *call(functools.partial(input_y_kernel, plan), "input_y", [msg] * 2, buffers, (*parts, *xr), 1000)
    )

    work = [pltpu.VMEM(plan.padded(19), f32), pltpu.VMEM(padded, f32)]
    work.append(pltpu.VMEM((3, tiles, nx, plan.rows, lanes), f32))

    def x_message(last_phase):
        return (tiles, plan.x_layout(last_phase)["rows"], lanes)

    def y_message(last_phase):
        return (tiles, plan.y_layout(last_phase)["rows"], lanes)

    pops = (19, *field)
    outs = [plan.padded(plan.n_state), (18, *field), (3 * (steps - 1), *field), pops, padded]
    outs += [x_message(False)] * 2 + [y_message(False)] * 2
    state, solid, vels, a, kext, xa, xb, up, down = call(
        functools.partial(first_kernel, plan), "first", outs, work, (*parts, *xr, *yr), 100000
    )
    grad = None
    for s in reversed(range(steps - 1)):
        xr = along_x(xa, xb)
        msg = y_message(False)
        ksum, ya, yb = call(
            functools.partial(y_kernel, plan, False),
            f"rows_{s}",
            [padded, msg, msg],
            [pltpu.VMEM(msg, f32)] * 2,
            (kext, *xr, up, down),
            1000,
        )
        yr = along_y(ya, yb)
        args = [state, solid, vels, a, ksum, *xr, *yr]
        if grad is not None:
            args.append(grad)
        scratch = work + [pltpu.VMEM(padded, f32)]
        if s > 0:
            outs = [pops, padded] + [x_message(False)] * 2 + [y_message(False)] * 2 + [field]
        else:
            outs = [(19, nx, ny, lanes)] * n + [padded] + [x_message(True)] * 2 + [field]
            scratch = scratch + [pltpu.VMEM((tiles, 19, nx, ny, lanes), f32)]
        res = call(
            functools.partial(next_kernel, plan, s, grad is not None), f"next_{s}", outs, scratch, args, 100000
        )
        if s > 0:
            a, kext, xa, xb, up, down, grad = res
        else:
            a_parts, (kext, xa, xb, grad) = res[:n], res[n:]

    a_parts = within_gz(a_parts)
    xr = along_x(xa, xb)
    msg = y_message(True)
    ksum, ya, yb = call(
        functools.partial(y_kernel, plan, True),
        "rows_end",
        [padded, msg, msg],
        [pltpu.VMEM(msg, f32)] * 2,
        (kext, *xr),
        1000,
    )
    yr = along_y(ya, yb)
    both = (2, nx, ny, lanes)
    r_parts = call(
        functools.partial(close_kernel, plan),
        "close",
        [both] * n,
        [pltpu.VMEM(padded, f32), pltpu.VMEM((tiles, *both), f32)],
        (state, ksum, *yr, grad),
        1000,
    )
    r_parts = within_gz(r_parts)
    out, gradient = call(
        functools.partial(join_kernel, plan),
        "join",
        [cotangent.shape, adhesion.shape],
        [],
        (*a_parts, *r_parts),
        1000,
    )
    return out, gradient


def solution(mesh):
    return jax.shard_map(
        per_device,
        mesh=mesh,
        in_specs=(
            P(None, "gx", "gy", "gz"),
            P(None, "gx", "gy", "gz"),
            P(None, None, "gx", "gy", "gz"),
            P("gx", "gy", "gz"),
            P("gx", "gy", "gz"),
        ),
        out_specs=(P(None, "gx", "gy", "gz"), P("gx", "gy", "gz")),
        check_vma=False,
    )
```

profile of v0, /device:TPU:0, one launch (start us, length us, event | category | flops | bytes accessed | tf_op | source)
XLA Modules:
  0.0 68.3 jit_solution(1784560325068950966)
XLA Ops:
  0.6 1.3 %copy-done = f32[19,8,16,128]{3,2,1,0:T(8,128)S(1)} copy-done((f32[19,8,16,128]{3,2,1,0:T(8,128)S(1)}, f32[19,8,16,128]{3,2,1,0:T(8,128)}, u32[]{:S(2)}) %copy-start) | copy-done | bytes 1245208
  6.9 2.3 %collective-permute-done.refs_1_ = f32[33,4,16,128]{3,2,1,0:T(8,128)S(1)} collective-permute-done((f32[33,4,16,128]{3,2,1,0:T(8,128)S(1)}, f32[33,4,16,128]{3,2,1,0:T(8,128)S(1)}, u32[]{:S(2)}, u32[]{:S(2)}) %collective-permute-start) | collective-permute-done | bytes 1081376 | tf_op jit(solution)/shard_map/ppermute | solution.py:724
  9.7 4.7 %collective-permute-start.2 = (f32[10,2,16,128]{3,2,1,0:T(8,128)S(1)}, f32[10,2,16,128]{3,2,1,0:T(8,128)S(1)}, u32[]{:S(2)}, u32[]{:S(2)}) collective-permute-start(f32[10,2,16,128]{3,2,1,0:T(8,128)S(1)} %get-tuple-element.44), channel_id=1, source_target_pairs={{0,25},{1,8},{8,1},{9,16},{16,9},{17,24},{24,17},{25,0},{2,27},{3,... | collective-permute-start | bytes 491528 | tf_op jit(solution)/shard_map/ppermute | solution.py:691
  14.4 4.0 %collective-permute-done.2.refs_3_ = f32[10,2,16,128]{3,2,1,0:T(8,128)S(1)} collective-permute-done((f32[10,2,16,128]{3,2,1,0:T(8,128)S(1)}, f32[10,2,16,128]{3,2,1,0:T(8,128)S(1)}, u32[]{:S(2)}, u32[]{:S(2)}) %collective-permute-start.2) | collective-permute-done | bytes 163872 | tf_op jit(solution)/shard_map/ppermute | solution.py:691
  18.6 1.6 %collective-permute-start.3 = (f32[2,56,128]{2,1,0:T(8,128)S(1)}, f32[2,56,128]{2,1,0:T(8,128)S(1)}, u32[]{:S(2)}, u32[]{:S(2)}) collective-permute-start(f32[2,56,128]{2,1,0:T(8,128)S(1)} %get-tuple-element.45), channel_id=1, source_target_pairs={{0,2},{2,0},{4,6},{6,4},{1,3},{3,1},{5,7},{7,5},{8,10},{10,8},{12,... | collective-permute-start | bytes 172040 | tf_op jit(solution)/shard_map/ppermute | solution.py:691
  20.1 1.5 %collective-permute-start.4 = (f32[2,56,128]{2,1,0:T(8,128)S(1)}, f32[2,56,128]{2,1,0:T(8,128)S(1)}, u32[]{:S(2)}, u32[]{:S(2)}) collective-permute-start(f32[2,56,128]{2,1,0:T(8,128)S(1)} %get-tuple-element.46), channel_id=1, source_target_pairs={{0,6},{2,4},{4,2},{6,0},{1,7},{3,5},{5,3},{7,1},{8,14},{10,12},{12... | collective-permute-start | bytes 172040 | tf_op jit(solution)/shard_map/ppermute | solution.py:691
  21.6 1.6 %collective-permute-done.3.refs_4_ = f32[2,56,128]{2,1,0:T(8,128)S(1)} collective-permute-done((f32[2,56,128]{2,1,0:T(8,128)S(1)}, f32[2,56,128]{2,1,0:T(8,128)S(1)}, u32[]{:S(2)}, u32[]{:S(2)}) %collective-permute-start.3) | collective-permute-done | bytes 57376 | tf_op jit(solution)/shard_map/ppermute | solution.py:691
  23.2 2.0 %collective-permute-done.4.refs_5_ = f32[2,56,128]{2,1,0:T(8,128)S(1)} collective-permute-done((f32[2,56,128]{2,1,0:T(8,128)S(1)}, f32[2,56,128]{2,1,0:T(8,128)S(1)}, u32[]{:S(2)}, u32[]{:S(2)}) %collective-permute-start.4) | collective-permute-done | bytes 57376 | tf_op jit(solution)/shard_map/ppermute | solution.py:691
  25.2 1.5 %first.1 = (f32[5,2,6,32,128]{4,3,2,1,0:T(8,128)S(1)}, f32[18,2,4,16,128]{4,3,2,1,0:T(8,128)S(1)}, f32[6,2,4,16,128]{4,3,2,1,0:T(8,128)S(1)}, f32[19,2,4,16,128]...) custom-call(f32[33,4,16,128]{3,2,1,0:T(8,128)S(1)} %get-tuple-elemen, ...), custom_call_target="tpu_custom_call" | custom-call | flops 100000 | tf_op jit(solution)/shard_map/first/pallas_call | solution.py:696
  26.8 1.3 %collective-permute-start.6 = (f32[2,120,128]{2,1,0:T(8,128)S(1)}, f32[2,120,128]{2,1,0:T(8,128)S(1)}, u32[]{:S(2)}, u32[]{:S(2)}) collective-permute-start(f32[2,120,128]{2,1,0:T(8,128)S(1)} %get-tuple-element.53), channel_id=1, source_target_pairs={{0,25},{1,8},{8,1},{9,16},{16,9},{17,24},{24,17},{25,0},{2,27},{3,... | collective-permute-start | bytes 368648 | tf_op jit(solution)/shard_map/ppermute | solution.py:691
  28.1 5.0 %collective-permute-done.6.refs_2_.refs_6_ = f32[2,120,128]{2,1,0:T(8,128)S(1)} collective-permute-done((f32[2,120,128]{2,1,0:T(8,128)S(1)}, f32[2,120,128]{2,1,0:T(8,128)S(1)}, u32[]{:S(2)}, u32[]{:S(2)}) %collective-permute-start.6) | collective-permute-done | bytes 122912 | tf_op jit(solution)/shard_map/ppermute | solution.py:691
  33.1 1.3 %collective-permute-start.7 = (f32[2,40,128]{2,1,0:T(8,128)S(1)}, f32[2,40,128]{2,1,0:T(8,128)S(1)}, u32[]{:S(2)}, u32[]{:S(2)}) collective-permute-start(f32[2,40,128]{2,1,0:T(8,128)S(1)} %get-tuple-element.57), channel_id=1, source_target_pairs={{0,2},{2,0},{4,6},{6,4},{1,3},{3,1},{5,7},{7,5},{8,10},{10,8},{12,... | collective-permute-start | bytes 122888 | tf_op jit(solution)/shard_map/ppermute | solution.py:691
  34.4 1.7 %collective-permute-start.8 = (f32[2,40,128]{2,1,0:T(8,128)S(1)}, f32[2,40,128]{2,1,0:T(8,128)S(1)}, u32[]{:S(2)}, u32[]{:S(2)}) collective-permute-start(f32[2,40,128]{2,1,0:T(8,128)S(1)} %get-tuple-element.58), channel_id=1, source_target_pairs={{0,6},{2,4},{4,2},{6,0},{1,7},{3,5},{5,3},{7,1},{8,14},{10,12},{12... | collective-permute-start | bytes 122888 | tf_op jit(solution)/shard_map/ppermute | solution.py:691
  37.2 2.2 %collective-permute-done.8.refs_8_ = f32[2,40,128]{2,1,0:T(8,128)S(1)} collective-permute-done((f32[2,40,128]{2,1,0:T(8,128)S(1)}, f32[2,40,128]{2,1,0:T(8,128)S(1)}, u32[]{:S(2)}, u32[]{:S(2)}) %collective-permute-start.8) | collective-permute-done | bytes 40992 | tf_op jit(solution)/shard_map/ppermute | solution.py:691
  42.0 4.9 %collective-permute-done.10.refs_2_.refs_6_ = f32[2,120,128]{2,1,0:T(8,128)S(1)} collective-permute-done((f32[2,120,128]{2,1,0:T(8,128)S(1)}, f32[2,120,128]{2,1,0:T(8,128)S(1)}, u32[]{:S(2)}, u32[]{:S(2)}) %collective-permute-start.10) | collective-permute-done | bytes 122912 | tf_op jit(solution)/shard_map/ppermute | solution.py:691
  47.9 1.5 %collective-permute-start.12 = (f32[2,40,128]{2,1,0:T(8,128)S(1)}, f32[2,40,128]{2,1,0:T(8,128)S(1)}, u32[]{:S(2)}, u32[]{:S(2)}) collective-permute-start(f32[2,40,128]{2,1,0:T(8,128)S(1)} %get-tuple-element.67), channel_id=1, source_target_pairs={{0,6},{2,4},{4,2},{6,0},{1,7},{3,5},{5,3},{7,1},{8,14},{10,12},{12... | collective-permute-start | bytes 122888 | tf_op jit(solution)/shard_map/ppermute | solution.py:691
  49.4 1.7 %collective-permute-done.11.refs_7_ = f32[2,40,128]{2,1,0:T(8,128)S(1)} collective-permute-done((f32[2,40,128]{2,1,0:T(8,128)S(1)}, f32[2,40,128]{2,1,0:T(8,128)S(1)}, u32[]{:S(2)}, u32[]{:S(2)}) %collective-permute-start.11) | collective-permute-done | bytes 40992 | tf_op jit(solution)/shard_map/ppermute | solution.py:691
  51.1 1.7 %collective-permute-done.12.refs_8_ = f32[2,40,128]{2,1,0:T(8,128)S(1)} collective-permute-done((f32[2,40,128]{2,1,0:T(8,128)S(1)}, f32[2,40,128]{2,1,0:T(8,128)S(1)}, u32[]{:S(2)}, u32[]{:S(2)}) %collective-permute-start.12) | collective-permute-done | bytes 40992 | tf_op jit(solution)/shard_map/ppermute | solution.py:691
  52.8 1.4 %next_0.1 = (f32[19,4,16,128]{3,2,1,0:T(8,128)S(1)}, f32[19,4,16,128]{3,2,1,0:T(8,128)S(1)}, f32[2,6,32,128]{3,2,1,0:T(8,128)S(1)}, f32[2,24,128]{2,1,0:T(8,128)...) custom-call(f32[5,2,6,32,128]{4,3,2,1,0:T(8,128)S(1)} %get-tuple-element.47.refs_0_.state, ...), custom_call_target="tpu_custom_call" | custom-call | flops 100000 | tf_op jit(solution)/shard_map/next_0/pallas_call | solution.py:696
  54.8 1.6 %collective-permute-done.14.refs_1_ = f32[2,24,128]{2,1,0:T(8,128)S(1)} collective-permute-done((f32[2,24,128]{2,1,0:T(8,128)S(1)}, f32[2,24,128]{2,1,0:T(8,128)S(1)}, u32[]{:S(2)}, u32[]{:S(2)}) %collective-permute-start.14) | collective-permute-done | bytes 24608 | tf_op jit(solution)/shard_map/ppermute | solution.py:691
  56.4 3.5 %collective-permute-done.15.refs_2_ = f32[2,24,128]{2,1,0:T(8,128)S(1)} collective-permute-done((f32[2,24,128]{2,1,0:T(8,128)S(1)}, f32[2,24,128]{2,1,0:T(8,128)S(1)}, u32[]{:S(2)}, u32[]{:S(2)}) %collective-permute-start.15) | collective-permute-done | bytes 24608 | tf_op jit(solution)/shard_map/ppermute | solution.py:691
  59.9 1.3 %collective-permute-start.16 = (f32[2,8,128]{2,1,0:T(8,128)S(1)}, f32[2,8,128]{2,1,0:T(8,128)S(1)}, u32[]{:S(2)}, u32[]{:S(2)}) collective-permute-start(f32[2,8,128]{2,1,0:T(8,128)S(1)} %get-tuple-element.75), channel_id=1, source_target_pairs={{0,2},{2,0},{4,6},{6,4},{1,3},{3,1},{5,7},{7,5},{8,10},{10,8},{12,... | collective-permute-start | bytes 24584 | tf_op jit(solution)/shard_map/ppermute | solution.py:691
  61.2 1.7 %collective-permute-start.17 = (f32[2,8,128]{2,1,0:T(8,128)S(1)}, f32[2,8,128]{2,1,0:T(8,128)S(1)}, u32[]{:S(2)}, u32[]{:S(2)}) collective-permute-start(f32[2,8,128]{2,1,0:T(8,128)S(1)} %get-tuple-element.76), channel_id=1, source_target_pairs={{0,6},{2,4},{4,2},{6,0},{1,7},{3,5},{5,3},{7,1},{8,14},{10,12},{12... | collective-permute-start | bytes 24584 | tf_op jit(solution)/shard_map/ppermute | solution.py:691
  63.6 2.2 %collective-permute-done.17.yr_b = f32[2,8,128]{2,1,0:T(8,128)S(1)} collective-permute-done((f32[2,8,128]{2,1,0:T(8,128)S(1)}, f32[2,8,128]{2,1,0:T(8,128)S(1)}, u32[]{:S(2)}, u32[]{:S(2)}) %collective-permute-start.17) | collective-permute-done | bytes 8224 | tf_op jit(solution)/shard_map/ppermute | solution.py:691
  (35 shorter events, 14.1 us)
Async XLA Ops:
  0.6 1.3 %copy-start = (f32[19,8,16,128]{3,2,1,0:T(8,128)S(1)}, f32[19,8,16,128]{3,2,1,0:T(8,128)}, u32[]{:S(2)}) copy-start(f32[19,8,16,128]{3,2,1,0:T(8,128)} %cot.1) | copy-start | bytes 3735556
  1.9 1.1 %copy-start.1 = (f32[3,3,8,16,128]{4,3,2,1,0:T(8,128)S(1)}, f32[3,3,8,16,128]{4,3,2,1,0:T(8,128)}, u32[]{:S(2)}) copy-start(f32[3,3,8,16,128]{4,3,2,1,0:T(8,128)} %vel.1) | copy-start | bytes 1769476
  3.0 0.9 %copy-start.2 = (f32[3,8,16,128]{3,2,1,0:T(8,128)S(1)}, f32[3,8,16,128]{3,2,1,0:T(8,128)}, u32[]{:S(2)}) copy-start(f32[3,8,16,128]{3,2,1,0:T(8,128)} %dens.1) | copy-start | bytes 589828
  3.9 0.8 %copy-start.3 = (f32[8,16,128]{2,1,0:T(8,128)S(1)}, f32[8,16,128]{2,1,0:T(8,128)}, u32[]{:S(2)}) copy-start(f32[8,16,128]{2,1,0:T(8,128)} %adh.1) | copy-start | bytes 196612
  4.8 0.8 %copy-start.4 = (s32[8,16,128]{2,1,0:T(8,128)S(1)}, s32[8,16,128]{2,1,0:T(8,128)}, u32[]{:S(2)}) copy-start(s32[8,16,128]{2,1,0:T(8,128)} %fluid.1) | copy-start | bytes 196612
  6.3 2.9 %collective-permute-start = (f32[33,4,16,128]{3,2,1,0:T(8,128)S(1)}, f32[33,4,16,128]{3,2,1,0:T(8,128)S(1)}, u32[]{:S(2)}, u32[]{:S(2)}) collective-permute-start(f32[33,4,16,128]{3,2,1,0:T(8,128)S(1)} %get-tuple-element.42), channel_id=1, source_target_pairs={{0,1},{1,0},{2,3},{3,2},{4,5},{5,4},{6,7},{7,6},{8,9},{9,8},{10,11... | collective-permute-start | bytes 3244040 | tf_op jit(solution)/shard_map/ppermute | solution.py:724
  9.3 5.1 %collective-permute-start.1 = (f32[10,2,16,128]{3,2,1,0:T(8,128)S(1)}, f32[10,2,16,128]{3,2,1,0:T(8,128)S(1)}, u32[]{:S(2)}, u32[]{:S(2)}) collective-permute-start(f32[10,2,16,128]{3,2,1,0:T(8,128)S(1)} %get-tuple-element.43), channel_id=1, source_target_pairs={{0,1},{1,0},{8,9},{9,8},{16,17},{17,16},{24,25},{25,24},{2,3},{3,2... | collective-permute-start | bytes 491528 | tf_op jit(solution)/shard_map/ppermute | solution.py:691
  9.7 8.7 %collective-permute-start.2 = (f32[10,2,16,128]{3,2,1,0:T(8,128)S(1)}, f32[10,2,16,128]{3,2,1,0:T(8,128)S(1)}, u32[]{:S(2)}, u32[]{:S(2)}) collective-permute-start(f32[10,2,16,128]{3,2,1,0:T(8,128)S(1)} %get-tuple-element.44), channel_id=1, source_target_pairs={{0,25},{1,8},{8,1},{9,16},{16,9},{17,24},{24,17},{25,0},{2,27},{3,... | collective-permute-start | bytes 491528 | tf_op jit(solution)/shard_map/ppermute | solution.py:691
  18.6 4.6 %collective-permute-start.3 = (f32[2,56,128]{2,1,0:T(8,128)S(1)}, f32[2,56,128]{2,1,0:T(8,128)S(1)}, u32[]{:S(2)}, u32[]{:S(2)}) collective-permute-start(f32[2,56,128]{2,1,0:T(8,128)S(1)} %get-tuple-element.45), channel_id=1, source_target_pairs={{0,2},{2,0},{4,6},{6,4},{1,3},{3,1},{5,7},{7,5},{8,10},{10,8},{12,... | collective-permute-start | bytes 172040 | tf_op jit(solution)/shard_map/ppermute | solution.py:691
  20.1 5.1 %collective-permute-start.4 = (f32[2,56,128]{2,1,0:T(8,128)S(1)}, f32[2,56,128]{2,1,0:T(8,128)S(1)}, u32[]{:S(2)}, u32[]{:S(2)}) collective-permute-start(f32[2,56,128]{2,1,0:T(8,128)S(1)} %get-tuple-element.46), channel_id=1, source_target_pairs={{0,6},{2,4},{4,2},{6,0},{1,7},{3,5},{5,3},{7,1},{8,14},{10,12},{12... | collective-permute-start | bytes 172040 | tf_op jit(solution)/shard_map/ppermute | solution.py:691
  26.7 1.4 %collective-permute-start.5 = (f32[2,120,128]{2,1,0:T(8,128)S(1)}, f32[2,120,128]{2,1,0:T(8,128)S(1)}, u32[]{:S(2)}, u32[]{:S(2)}) collective-permute-start(f32[2,120,128]{2,1,0:T(8,128)S(1)} %get-tuple-element.52), channel_id=1, source_target_pairs={{0,1},{1,0},{8,9},{9,8},{16,17},{17,16},{24,25},{25,24},{2,3},{3,2... | collective-permute-start | bytes 368648 | tf_op jit(solution)/shard_map/ppermute | solution.py:691
  26.8 6.3 %collective-permute-start.6 = (f32[2,120,128]{2,1,0:T(8,128)S(1)}, f32[2,120,128]{2,1,0:T(8,128)S(1)}, u32[]{:S(2)}, u32[]{:S(2)}) collective-permute-start(f32[2,120,128]{2,1,0:T(8,128)S(1)} %get-tuple-element.53), channel_id=1, source_target_pairs={{0,25},{1,8},{8,1},{9,16},{16,9},{17,24},{24,17},{25,0},{2,27},{3,... | collective-permute-start | bytes 368648 | tf_op jit(solution)/shard_map/ppermute | solution.py:691
  33.1 4.1 %collective-permute-start.7 = (f32[2,40,128]{2,1,0:T(8,128)S(1)}, f32[2,40,128]{2,1,0:T(8,128)S(1)}, u32[]{:S(2)}, u32[]{:S(2)}) collective-permute-start(f32[2,40,128]{2,1,0:T(8,128)S(1)} %get-tuple-element.57), channel_id=1, source_target_pairs={{0,2},{2,0},{4,6},{6,4},{1,3},{3,1},{5,7},{7,5},{8,10},{10,8},{12,... | collective-permute-start | bytes 122888 | tf_op jit(solution)/shard_map/ppermute | solution.py:691
  34.4 4.9 %collective-permute-start.8 = (f32[2,40,128]{2,1,0:T(8,128)S(1)}, f32[2,40,128]{2,1,0:T(8,128)S(1)}, u32[]{:S(2)}, u32[]{:S(2)}) collective-permute-start(f32[2,40,128]{2,1,0:T(8,128)S(1)} %get-tuple-element.58), channel_id=1, source_target_pairs={{0,6},{2,4},{4,2},{6,0},{1,7},{3,5},{5,3},{7,1},{8,14},{10,12},{12... | collective-permute-start | bytes 122888 | tf_op jit(solution)/shard_map/ppermute | solution.py:691
  40.6 1.4 %collective-permute-start.9 = (f32[2,120,128]{2,1,0:T(8,128)S(1)}, f32[2,120,128]{2,1,0:T(8,128)S(1)}, u32[]{:S(2)}, u32[]{:S(2)}) collective-permute-start(f32[2,120,128]{2,1,0:T(8,128)S(1)} %get-tuple-element.61), channel_id=1, source_target_pairs={{0,1},{1,0},{8,9},{9,8},{16,17},{17,16},{24,25},{25,24},{2,3},{3,2... | collective-permute-start | bytes 368648 | tf_op jit(solution)/shard_map/ppermute | solution.py:691
  40.7 6.3 %collective-permute-start.10 = (f32[2,120,128]{2,1,0:T(8,128)S(1)}, f32[2,120,128]{2,1,0:T(8,128)S(1)}, u32[]{:S(2)}, u32[]{:S(2)}) collective-permute-start(f32[2,120,128]{2,1,0:T(8,128)S(1)} %get-tuple-element.62), channel_id=1, source_target_pairs={{0,25},{1,8},{8,1},{9,16},{16,9},{17,24},{24,17},{25,0},{2,27},{3,... | collective-permute-start | bytes 368648 | tf_op jit(solution)/shard_map/ppermute | solution.py:691
  47.0 4.1 %collective-permute-start.11 = (f32[2,40,128]{2,1,0:T(8,128)S(1)}, f32[2,40,128]{2,1,0:T(8,128)S(1)}, u32[]{:S(2)}, u32[]{:S(2)}) collective-permute-start(f32[2,40,128]{2,1,0:T(8,128)S(1)} %get-tuple-element.66), channel_id=1, source_target_pairs={{0,2},{2,0},{4,6},{6,4},{1,3},{3,1},{5,7},{7,5},{8,10},{10,8},{12,... | collective-permute-start | bytes 122888 | tf_op jit(solution)/shard_map/ppermute | solution.py:691
  47.9 4.9 %collective-permute-start.12 = (f32[2,40,128]{2,1,0:T(8,128)S(1)}, f32[2,40,128]{2,1,0:T(8,128)S(1)}, u32[]{:S(2)}, u32[]{:S(2)}) collective-permute-start(f32[2,40,128]{2,1,0:T(8,128)S(1)} %get-tuple-element.67), channel_id=1, source_target_pairs={{0,6},{2,4},{4,2},{6,0},{1,7},{3,5},{5,3},{7,1},{8,14},{10,12},{12... | collective-permute-start | bytes 122888 | tf_op jit(solution)/shard_map/ppermute | solution.py:691
  54.2 12.9 %collective-permute-start.13 = (f32[19,4,16,128]{3,2,1,0:T(8,128)S(1)}, f32[19,4,16,128]{3,2,1,0:T(8,128)S(1)}, u32[]{:S(2)}, u32[]{:S(2)}) collective-permute-start(f32[19,4,16,128]{3,2,1,0:T(8,128)S(1)} %get-tuple-element.70), channel_id=1, source_target_pairs={{0,1},{1,0},{2,3},{3,2},{4,5},{5,4},{6,7},{7,6},{8,9},{9,8},{10,11... | collective-permute-start | bytes 1867784 | tf_op jit(solution)/shard_map/ppermute | solution.py:724
  54.3 2.1 %collective-permute-start.14 = (f32[2,24,128]{2,1,0:T(8,128)S(1)}, f32[2,24,128]{2,1,0:T(8,128)S(1)}, u32[]{:S(2)}, u32[]{:S(2)}) collective-permute-start(f32[2,24,128]{2,1,0:T(8,128)S(1)} %get-tuple-element.72), channel_id=1, source_target_pairs={{0,1},{1,0},{8,9},{9,8},{16,17},{17,16},{24,25},{25,24},{2,3},{3,2... | collective-permute-start | bytes 73736 | tf_op jit(solution)/shard_map/ppermute | solution.py:691
  54.8 5.0 %collective-permute-start.15 = (f32[2,24,128]{2,1,0:T(8,128)S(1)}, f32[2,24,128]{2,1,0:T(8,128)S(1)}, u32[]{:S(2)}, u32[]{:S(2)}) collective-permute-start(f32[2,24,128]{2,1,0:T(8,128)S(1)} %get-tuple-element.73), channel_id=1, source_target_pairs={{0,25},{1,8},{8,1},{9,16},{16,9},{17,24},{24,17},{25,0},{2,27},{3,... | collective-permute-start | bytes 73736 | tf_op jit(solution)/shard_map/ppermute | solution.py:691
  59.9 3.7 %collective-permute-start.16 = (f32[2,8,128]{2,1,0:T(8,128)S(1)}, f32[2,8,128]{2,1,0:T(8,128)S(1)}, u32[]{:S(2)}, u32[]{:S(2)}) collective-permute-start(f32[2,8,128]{2,1,0:T(8,128)S(1)} %get-tuple-element.75), channel_id=1, source_target_pairs={{0,2},{2,0},{4,6},{6,4},{1,3},{3,1},{5,7},{7,5},{8,10},{10,8},{12,... | collective-permute-start | bytes 24584 | tf_op jit(solution)/shard_map/ppermute | solution.py:691
  61.2 4.5 %collective-permute-start.17 = (f32[2,8,128]{2,1,0:T(8,128)S(1)}, f32[2,8,128]{2,1,0:T(8,128)S(1)}, u32[]{:S(2)}, u32[]{:S(2)}) collective-permute-start(f32[2,8,128]{2,1,0:T(8,128)S(1)} %get-tuple-element.76), channel_id=1, source_target_pairs={{0,6},{2,4},{4,2},{6,0},{1,7},{3,5},{5,3},{7,1},{8,14},{10,12},{12... | collective-permute-start | bytes 24584 | tf_op jit(solution)/shard_map/ppermute | solution.py:691
  65.8 1.3 %collective-permute-start.18 = (f32[2,4,16,128]{3,2,1,0:T(8,128)S(1)}, f32[2,4,16,128]{3,2,1,0:T(8,128)S(1)}, u32[]{:S(2)}, u32[]{:S(2)}) collective-permute-start(f32[2,4,16,128]{3,2,1,0:T(8,128)S(1)} %get-tuple-element.79), channel_id=1, source_target_pairs={{0,1},{1,0},{2,3},{3,2},{4,5},{5,4},{6,7},{7,6},{8,9},{9,8},{10,11... | collective-permute-start | bytes 196616 | tf_op jit(solution)/shard_map/ppermute | solution.py:724
where the time goes:
time: 68.6 us; the launch traced here: 68.3 us
  waiting for transfers between devices  36.8 us (54%)
  starting transfers between devices  19.3 us (28%)
  Pallas kernels  6.47 us (9%)
  local copies, waits for them, and re-layouts  4.95 us (7%)
  between operations  0.74 us (1%)
    ppermute x16, waiting for transfers between devices, swap_along(): return (lax.ppermute(first, axes, one), lax.ppermute(second, axes, two))  33.2 us
    ppermute x16, starting transfers between devices, swap_along(): return (lax.ppermute(first, axes, one), lax.ppermute(second, axes, two))  18.6 us
    pallas_call x11, Pallas kernels, call(): pl.pallas_call(kernel, name=name, out_shape=tuple((jax.ShapeDtypeStruct(s...  6.47 us
    unnamed x10, local copies, waits for them, and re-layouts  4.95 us
    ppermute x3, waiting for transfers between devices, within_gz(): lax.ppermute(parts[d], 'gz', [(i, (i + d) % n) for i in range(n)])  3.58 us
  transfers between devices with their start and end apart: 19, of which 16 were waited for; matrix products, arithmetic and copies ran while one was open for 0% of the time, Pallas kernels for 0%

commit v1 on v0

--- a/solution.py
+++ b/solution.py
@@ -56,7 +56,7 @@
         self.steps = steps
         self.chain_x = n_gx * n_gz
         self.chain_y = n_gy
-        self.n_gz = n_gz
+        self.n_gx, self.n_gy, self.n_gz = n_gx, n_gy, n_gz
         self.q_rho = 19
         self.q_vel = 19 + steps
         self.q_adh = 19 + 4 * steps
@@ -66,6 +66,8 @@
         self.s_adh = steps
         self.s_fl = steps + 1
         self.rows = self.ny + 2 * PAD
+        self.in_rows = -(-(5 + self.n_state) // 8) * 8
+        self.in_ends = -(-(2 * self.n_state + 2) // 8) * 8
 
     def padded(self, count):
         return (count, self.tiles, self.nx + 2, self.rows, self.lanes)
@@ -95,11 +97,6 @@
         out["rows"] = -(-at // 8) * 8
         return out
 
-    def input_y_layout(self):
-        pops = self.n_state * (self.nx + 2)
-        edges = pops + 5 * self.nx
-        return {"pops": pops, "edges": edges, "rows": -(-(edges + 2) // 8) * 8}
-
 
 def flag(cond, shape):
     return jnp.full(shape, cond.astype(jnp.int32), jnp.int32) == 1
@@ -143,12 +140,12 @@
 
 def split_kernel(plan, cot, dens, vel, adh, fluid, *rest):
     n = plan.n_gz
-    outs = rest[:n]
-    whole, sems = rest[n], rest[n + 1]
+    outs, (out_a, out_b) = rest[:n], rest[n : n + 2]
+    whole, up, down, sems = rest[n + 2 :]
     me = lax.axis_index("gz")
-    nx = plan.nx
+    nx, ny = plan.nx, plan.ny
     copies = []
-    for k, d in enumerate(list(range(1, n)) + [0]):
+    for d in range(n):
         chunk = pl.ds(lax.rem(me + d, n) * nx, nx)
         out = outs[d]
         pairs = [
@@ -160,14 +157,40 @@
         for s in range(plan.steps):
             at = plan.q_vel + 3 * s
             pairs.append((vel.at[s, :, chunk], out.at[at : at + 3]))
-        for j, (src, dst) in enumerate(pairs):
-            copies.append(pltpu.make_async_copy(src, dst, sems.at[k, j]))
+        for k, (src, dst) in enumerate(pairs):
+            copies.append(pltpu.make_async_copy(src, dst, sems.at[d, k]))
     for copy in copies:
         copy.start()
+    up[...] = jnp.zeros_like(up)
+    down[...] = jnp.zeros_like(down)
     for copy in copies:
         copy.wait()
     for d in range(n):
         outs[d][plan.q_fl] = whole[d].astype(jnp.float32)
+    even = chain_place("gy", plan.chain_y)[0]
+    for d in range(n):
+        start = lax.rem(me + d, n) * nx
+        for x in range(nx):
+            for k in range(5 + plan.n_state):
+                q = state_index(plan, k - 5)
+                up[0, k : k + 1] = outs[d][YM[k] if k < 5 else q, x, ny - 1 : ny]
+                down[0, k : k + 1] = outs[d][YP[k] if k < 5 else q, x, 0:1]
+            out_a[start + x] = pick(even, up[0], down[0])
+            out_b[start + x] = pick(even, down[0], up[0])
+
+
+def rows_kernel(plan, yr_a, yr_b, *outs):
+    n = plan.n_gz
+    me = lax.axis_index("gz")
+    nx, half = plan.nx, plan.in_rows
+    place = chain_place("gy", plan.chain_y)
+    for d in range(n):
+        start = lax.rem(me + d, n) * nx
+        for x in range(-1, nx + 1):
+            at = jnp.clip(start + x, 0, n * nx - 1)
+            plus, minus = halo_pair(place, yr_a[at], yr_b[at])
+            outs[d][x + 1, 0:half] = minus
+            outs[d][x + 1, half : 2 * half] = plus
 
 
 def tile_of(plan, refs, t, index):
@@ -186,34 +209,54 @@
 
 def input_x_kernel(plan, *refs):
     n = plan.n_gz
-    parts, (out_a, out_b) = refs[:n], refs[n:]
+    parts, rows, (out_a, out_b) = refs[:n], refs[n : 2 * n], refs[2 * n :]
     even = chain_place(X_AXES, plan.chain_x)[0]
-    for t in range(plan.tiles):
-        for j in range(5 + plan.n_state):
+    count, ny, half = 5 + plan.n_state, plan.ny, plan.in_rows
+    for t in range(plan.tiles):
+        for j in range(count):
             up = XM[j] if j < 5 else state_index(plan, j - 5)
             down = XP[j] if j < 5 else state_index(plan, j - 5)
             plus = tile_of(plan, parts, t, (up, plan.nx - 1))
             minus = tile_of(plan, parts, t, (down, 0))
-            out_a[j, t] = pick(even, plus, minus)
-            out_b[j, t] = pick(even, minus, plus)
-
-
-def input_y_kernel(plan, *refs):
-    n = plan.n_gz
-    parts = refs[:n]
-    xr_a, xr_b, out_a, out_b, up, down = refs[n:]
-    nx, ny = plan.nx, plan.ny
-    lay = plan.input_y_layout()
+            out_a[t, j * ny : (j + 1) * ny] = pick(even, plus, minus)
+            out_b[t, j * ny : (j + 1) * ny] = pick(even, minus, plus)
+        out_b[t, count * ny :] = jnp.zeros((plan.in_ends, plan.lanes), jnp.float32)
+        upper = tile_of(plan, rows, t, (plan.nx,))
+        lower = tile_of(plan, rows, t, (1,))
+        r = count * ny
+        for k in range(plan.n_state):
+            for shift in (0, half):
+                row = slice(shift + 5 + k, shift + 6 + k)
+                out_b[t, r : r + 1] = pick(even, lower[row], upper[row])
+                r += 1
+        for shift, side, moving in ((0, -1, YM), (half, 1, YP)):
+            row_up = shift + moving.index(EDGE[(-1, side)])
+            row_low = shift + moving.index(EDGE[(1, side)])
+            out_b[t, r : r + 1] = pick(even, lower[row_low : row_low + 1], upper[row_up : row_up + 1])
+            r += 1
+
+
+def fill_inputs(plan, parts, xr_a, xr_b, row_parts, state, apad):
+    nx, ny, half = plan.nx, plan.ny, plan.in_rows
+    count = 5 + plan.n_state
     place_x = chain_place(X_AXES, plan.chain_x)
-    even = chain_place("gy", plan.chain_y)[0]
-    up[...] = jnp.zeros_like(up)
-    down[...] = jnp.zeros_like(down)
-    top = slice(ny - 1, ny)
-    low = slice(0, 1)
-    for t in range(plan.tiles):
+    even, has_plus, has_minus = place_x
+    own = slice(PAD, PAD + ny)
+    first, last = slice(PAD - 1, PAD), slice(PAD + ny, PAD + ny + 1)
+    fl = plan.s_fl
+    for t in range(plan.tiles):
+        near = [tile_of(plan, row_parts, t, (x,)) for x in range(nx + 2)]
+        blank = jnp.zeros((1, plan.lanes), jnp.float32)
+
+        def beyond(side, row, r):
+            came = xr_b[t, count * ny + r : count * ny + r + 1]
+            if side > 0:
+                return pick(has_plus, pick(even, near[nx + 1][row : row + 1], came), blank)
+            return pick(has_minus, pick(even, came, near[0][row : row + 1]), blank)
+
         for k in range(plan.n_state):
-            base = k * (nx + 2)
-            plus, minus = halo_pair(place_x, xr_a[5 + k, t], xr_b[5 + k, t])
+            rows = slice((5 + k) * ny, (6 + k) * ny)
+            plus, minus = halo_pair(place_x, xr_a[t, rows], xr_b[t, rows])
             for x in range(-1, nx + 1):
                 if x < 0:
                     plane = minus
@@ -221,47 +264,14 @@
                     plane = plus
                 else:
                     plane = tile_of(plan, parts, t, (state_index(plan, k), x))
-                r = base + x + 1
-                up[t, r : r + 1] = plane[top]
-                down[t, r : r + 1] = plane[low]
-        for j in range(5):
-            for x in range(nx):
-                r = lay["pops"] + j * nx + x
-                up[t, r : r + 1] = tile_of(plan, parts, t, (YM[j], x, top))
-                down[t, r : r + 1] = tile_of(plan, parts, t, (YP[j], x, low))
-        r = lay["edges"]
-        for side, out, rows in ((-1, up, top), (1, down, low)):
-            j = XM.index(EDGE[(-1, side)])
-            out[t, r : r + 1] = halo_pair(place_x, xr_a[j, t], xr_b[j, t])[1][rows]
-            j = XP.index(EDGE[(1, side)])
-            out[t, r + 1 : r + 2] = halo_pair(place_x, xr_a[j, t], xr_b[j, t])[0][rows]
-        out_a[t] = pick(even, up[t], down[t])
-        out_b[t] = pick(even, down[t], up[t])
-
-
-def fill_inputs(plan, parts, xr_a, xr_b, yr_a, yr_b, state, apad):
-    nx, ny = plan.nx, plan.ny
-    lay = plan.input_y_layout()
-    place_x = chain_place(X_AXES, plan.chain_x)
-    place_y = chain_place("gy", plan.chain_y)
-    own = slice(PAD, PAD + ny)
-    first, last = slice(PAD - 1, PAD), slice(PAD + ny, PAD + ny + 1)
-    for t in range(plan.tiles):
-        y_plus, y_minus = halo_pair(place_y, yr_a[t], yr_b[t])
-        for k in range(plan.n_state):
-            plus, minus = halo_pair(place_x, xr_a[5 + k, t], xr_b[5 + k, t])
-            for x in range(-1, nx + 1):
-                if x < 0:
-                    plane = minus
-                elif x == nx:
-                    plane = plus
-                else:
-                    plane = tile_of(plan, parts, t, (state_index(plan, k), x))
-                r = k * (nx + 2) + x + 1
                 state[k, t, x + 1, own] = plane
-                state[k, t, x + 1, first] = y_minus[r : r + 1]
-                state[k, t, x + 1, last] = y_plus[r : r + 1]
-        fl = plan.s_fl
+                for shift, where, odd in ((0, first, 0), (half, last, 1)):
+                    row = shift + 5 + k
+                    if 0 <= x < nx:
+                        value = near[x + 1][row : row + 1]
+                    else:
+                        value = beyond(-1 if x < 0 else 1, row, 2 * k + odd)
+                    state[k, t, x + 1, where] = value
         for x in range(nx):
             mask = state[fl, t, x + 1, own]
             for i in range(19):
@@ -269,17 +279,20 @@
             mask_first = state[fl, t, x + 1, first]
             mask_last = state[fl, t, x + 1, last]
             for j in range(5):
-                r = lay["pops"] + j * nx + x
-                apad[YP[j], t, x + 1, last] = mask_last * y_plus[r : r + 1]
-                apad[YM[j], t, x + 1, first] = mask_first * y_minus[r : r + 1]
+                apad[YP[j], t, x + 1, last] = mask_last * near[x + 1][half + j : half + j + 1]
+                apad[YM[j], t, x + 1, first] = mask_first * near[x + 1][j : j + 1]
         for j in range(5):
-            plus, minus = halo_pair(place_x, xr_a[j, t], xr_b[j, t])
+            rows = slice(j * ny, (j + 1) * ny)
+            plus, minus = halo_pair(place_x, xr_a[t, rows], xr_b[t, rows])
             apad[XP[j], t, nx + 1, own] = state[fl, t, nx + 1, own] * plus
             apad[XM[j], t, 0, own] = state[fl, t, 0, own] * minus
-        r = lay["edges"]
-        for side, rows, msg in ((1, last, y_plus), (-1, first, y_minus)):
-            apad[EDGE[(-1, side)], t, 0, rows] = state[fl, t, 0, rows] * msg[r : r + 1]
-            apad[EDGE[(1, side)], t, nx + 1, rows] = state[fl, t, nx + 1, rows] * msg[r + 1 : r + 2]
+        for side, where, shift, moving, odd in ((-1, first, 0, YM, 0), (1, last, half, YP, 1)):
+            r = 2 * plan.n_state + odd
+            low, high = EDGE[(-1, side)], EDGE[(1, side)]
+            value = beyond(-1, shift + moving.index(low), r)
+            apad[low, t, 0, where] = state[fl, t, 0, where] * value
+            value = beyond(1, shift + moving.index(high), r)
+            apad[high, t, nx + 1, where] = state[fl, t, nx + 1, where] * value
 
 
 def complete_back(plan, last_phase, ksum, yr_a, yr_b, total):
@@ -547,12 +560,11 @@
 
 def first_kernel(plan, *refs):
     n = plan.n_gz
-    parts = refs[:n]
-    xr_a, xr_b, yr_a, yr_b = refs[n : n + 4]
-    state, solid, vels, a_ref, kext, out_a, out_b, up, down, apad, phi, vpad = refs[n + 4 :]
+    parts, row_parts, (xr_a, xr_b) = refs[:n], refs[n : 2 * n], refs[2 * n : 2 * n + 2]
+    state, solid, vels, a_ref, kext, out_a, out_b, up, down, apad, phi, vpad = refs[2 * n + 2 :]
     s = plan.steps - 1
     last_phase = s == 0
-    fill_inputs(plan, parts, xr_a, xr_b, yr_a, yr_b, state, apad)
+    fill_inputs(plan, parts, xr_a, xr_b, row_parts, state, apad)
     for t in range(plan.tiles):
         for k in range(3 * (plan.steps - 1)):
             vels[k, t] = tile_of(plan, parts, t, (plan.q_vel + k,))
@@ -680,19 +692,33 @@
         grad[chunk] = r_parts[d][1]
 
 
-def swaps(count):
-    one = [(i, i ^ 1) for i in range(count)]
-    two = [(i, (i + 1) % count if i % 2 else (i - 1) % count) for i in range(count)]
-    return one, two
-
-
-def swap_along(axes, count, first, second):
-    one, two = swaps(count)
-    return lax.ppermute(first, axes, one), lax.ppermute(second, axes, two)
+def swap_pairs(plan, along_gy, odd):
+    n_gx, n_gy, n_gz = plan.n_gx, plan.n_gy, plan.n_gz
+    out = []
+    for x in range(n_gx):
+        for y in range(n_gy):
+            for z in range(n_gz):
+                place, count = (y, n_gy) if along_gy else (x * n_gz + z, n_gx * n_gz)
+                other = place + 1 if place % 2 == odd else place - 1
+                to = (x, y, z)
+                if 0 <= other < count:
+                    to = (x, other, z) if along_gy else (other // n_gz, y, other % n_gz)
+                elif along_gy and n_gz % 2 == 0:
+                    to = (x, y, z ^ 1)
+                elif not along_gy and n_gy % 2 == 0:
+                    to = (x, y ^ 1, z)
+                out.append(((x * n_gy + y) * n_gz + z, (to[0] * n_gy + to[1]) * n_gz + to[2]))
+    return out
+
+
+def swap_along(plan, along_gy, first, second):
+    axes = ("gx", "gy", "gz")
+    late = lax.ppermute(second, axes, swap_pairs(plan, along_gy, 1))
+    return lax.ppermute(first, axes, swap_pairs(plan, along_gy, 0)), late
 
 
 def call(kernel, name, outs, scratch, args, flops, in_hbm=False):
-    spec = pl.BlockSpec(memory_space=pl.ANY if in_hbm else pltpu.VMEM)
+    spec = pl.BlockSpec(memory_space=pltpu.HBM if in_hbm else pltpu.VMEM)
     return pl.pallas_call(
         kernel,
         name=name,
@@ -702,7 +728,7 @@
         scratch_shapes=scratch,
         cost_estimate=pl.CostEstimate(flops=flops, bytes_accessed=0, transcendentals=0),
         compiler_params=pltpu.CompilerParams(vmem_limit_bytes=VMEM_LIMIT),
-    )(*args)
+    )(*[pltpu.with_memory_space_constraint(v, pltpu.HBM) if in_hbm else v for v in args])
 
 
 def per_device(cotangent, densities, velocities, adhesion, fluid):
@@ -714,10 +740,10 @@
     padded = plan.padded(1)[1:]
 
     def along_x(first, second):
-        return swap_along(X_AXES, plan.chain_x, first, second)
+        return swap_along(plan, False, first, second)
 
     def along_y(first, second):
-        return swap_along("gy", plan.chain_y, first, second)
+        return swap_along(plan, True, first, second)
 
     def within_gz(parts):
         return [parts[0]] + [
@@ -725,23 +751,26 @@
         ]
 
     part = (plan.nq, nx, ny, lanes)
-    parts = call(
+    half = plan.in_rows
+    msg = (n * nx, half, lanes)
+    scratch = [pltpu.VMEM((n, nx, ny, lanes), jnp.int32)] + [pltpu.VMEM((1, half, lanes), f32)] * 2
+    *parts, ya, yb = call(
         functools.partial(split_kernel, plan),
         "split",
-        [part] * n,
-        [pltpu.VMEM((n, nx, ny, lanes), jnp.int32), pltpu.SemaphoreType.DMA((n, 4 + steps))],
+        [part] * n + [msg] * 2,
+        scratch + [pltpu.SemaphoreType.DMA((n, 4 + steps))],
         (cotangent, densities, velocities, adhesion, fluid),
         1000,
         in_hbm=True,
     )
     parts = within_gz(parts)
-
-    msg = (5 + plan.n_state, tiles, ny, lanes)
-    xr = along_x(*call(functools.partial(input_x_kernel, plan), "input_x", [msg] * 2, [], parts, 1000))
-    msg = (tiles, plan.input_y_layout()["rows"], lanes)
-    buffers = [pltpu.VMEM(msg, f32)] * 2
-    yr = along_y(
-        *call(functools.partial(input_y_kernel, plan), "input_y", [msg] * 2, buffers, (*parts, *xr), 1000)
+    yr = along_y(ya, yb)
+    msg = (nx + 2, 2 * half, lanes)
+    row_parts = within_gz(call(functools.partial(rows_kernel, plan), "rows_in", [msg] * n, [], yr, 1000))
+    count = (5 + plan.n_state) * ny
+    msgs = [(tiles, count, lanes), (tiles, count + plan.in_ends, lanes)]
+    xr = along_x(
+        *call(functools.partial(input_x_kernel, plan), "input_x", msgs, [], (*parts, *row_parts), 1000)
     )
 
     work = [pltpu.VMEM(plan.padded(19), f32), pltpu.VMEM(padded, f32)]
@@ -757,7 +786,7 @@
     outs = [plan.padded(plan.n_state), (18, *field), (3 * (steps - 1), *field), pops, padded]
     outs += [x_message(False)] * 2 + [y_message(False)] * 2
     state, solid, vels, a, kext, xa, xb, up, down = call(
-        functools.partial(first_kernel, plan), "first", outs, work, (*parts, *xr, *yr), 100000
+        functools.partial(first_kernel, plan), "first", outs, work, (*parts, *row_parts, *xr), 100000
     )
     grad = None
     for s in reversed(range(steps - 1)):

time: 68.6 us -> 53 us (0.77)
  waiting for transfers between devices: 36.8 us -> 21.7 us
  local copies, waits for them, and re-layouts: 4.95 us -> 0 us
  starting transfers between devices: 19.3 us -> 22.7 us
  Pallas kernels: 6.47 us -> 7.44 us
    ppermute x16, waiting for transfers between devices: 33.2 us -> 19.2 us  [the longest x8 9.6 us: swap_along(): late = lax.ppermute(second, axes, swap_pairs(plan, along_gy, 1))]
    unnamed x10 -> x0, local copies, waits for them, and re-layouts: 4.95 us -> none
    ppermute x16, starting transfers between devices: 18.6 us -> 21.9 us  [the longest x8 12.5 us: swap_along(): late = lax.ppermute(second, axes, swap_pairs(plan, along_gy, 1))]
    ppermute x3 -> x4, waiting for transfers between devices: 3.58 us -> 2.53 us  [within_gz(): lax.ppermute(parts[d], 'gz', [(i, (i + d) % n) for i in range(n)])]
    pallas_call x11, Pallas kernels: 6.47 us -> 7.44 us  [call(): pl.pallas_call(kernel, name=name, out_shape=tuple((jax.ShapeDtypeStruct(s...]
  transfers between devices with their start and end apart: 19 -> 20, of which waited for: 16 -> 11; matrix products, arithmetic and copies ran while one was open for 0% -> 0% of each run, Pallas kernels for 0% -> 0%
where the time goes in v1:
time: 53 us; the launch traced here: 52.6 us
  starting transfers between devices  22.7 us (43%)
  waiting for transfers between devices  21.7 us (41%)
  Pallas kernels  7.44 us (14%)
  between operations  0.73 us (1%)
    ppermute x8, starting transfers between devices, swap_along(): late = lax.ppermute(second, axes, swap_pairs(plan, along_gy, 1))  12.5 us
    ppermute x8, waiting for transfers between devices, swap_along(): late = lax.ppermute(second, axes, swap_pairs(plan, along_gy, 1))  9.6 us
    ppermute x8, waiting for transfers between devices, swap_along(): return (lax.ppermute(first, axes, swap_pairs(plan, along_gy, 0)), late)  9.57 us
    ppermute x8, starting transfers between devices, swap_along(): return (lax.ppermute(first, axes, swap_pairs(plan, along_gy, 0)), late)  9.45 us
    pallas_call x11, Pallas kernels, call(): pl.pallas_call(kernel, name=name, out_shape=tuple((jax.ShapeDtypeStruct(s...  7.44 us
    ppermute x4, waiting for transfers between devices, within_gz(): lax.ppermute(parts[d], 'gz', [(i, (i + d) % n) for i in range(n)])  2.53 us
  transfers between devices with their start and end apart: 20, of which 11 were waited for; matrix products, arithmetic and copies ran while one was open for 0% of the time, Pallas kernels for 0%

profile of v1, /device:TPU:0, one launch (start us, length us, event | category | flops | bytes accessed | tf_op | source)
XLA Modules:
  0.0 52.6 jit_solution(295787443462021230)
XLA Ops:
  0.6 1.7 %split.1 = (f32[33,4,16,128]{3,2,1,0:T(8,128)S(1)}, f32[33,4,16,128]{3,2,1,0:T(8,128)S(1)}, f32[8,16,128]{2,1,0:T(8,128)S(1)}, f32[8,16,128]{2,1,0:T(8,128)S(1)}) custom-call(f32[19,8,16,128]{3,2,1,0:T(8,128)} %cot.1, f32[3,8,16,128]{3,2,1,0:T(8,128)} %dens.1, f32[3,3,8,16,128]{4,3,2,1,0:T(8,128)} %vel.1, f32[8,16,128]{2,1,0:T(8,128)} %adh.1, ...), custom_call_target="tpu_custom_call" | custom-call | flops 1000 | tf_op jit(solution)/shard_map/split/pallas_call | solution.py:722
  2.9 2.6 %collective-permute-start.1 = (f32[8,16,128]{2,1,0:T(8,128)S(1)}, f32[8,16,128]{2,1,0:T(8,128)S(1)}, u32[]{:S(2)}, u32[]{:S(2)}) collective-permute-start(f32[8,16,128]{2,1,0:T(8,128)S(1)} %get-tuple-element.45), channel_id=1, source_target_pairs={{0,2},{1,3},{2,0},{3,1},{4,6},{5,7},{6,4},{7,5},{8,10},{9,11},{10,... | collective-permute-start | bytes 196616 | tf_op jit(solution)/shard_map/ppermute | solution.py:717
  5.6 2.5 %collective-permute-done.1.yr_a = f32[8,16,128]{2,1,0:T(8,128)S(1)} collective-permute-done((f32[8,16,128]{2,1,0:T(8,128)S(1)}, f32[8,16,128]{2,1,0:T(8,128)S(1)}, u32[]{:S(2)}, u32[]{:S(2)}) %collective-permute-start.1) | collective-permute-done | bytes 65568 | tf_op jit(solution)/shard_map/ppermute | solution.py:717
  8.3 1.3 %collective-permute-done.3.refs_3_ = f32[6,32,128]{2,1,0:T(8,128)S(1)} collective-permute-done((f32[6,32,128]{2,1,0:T(8,128)S(1)}, f32[6,32,128]{2,1,0:T(8,128)S(1)}, u32[]{:S(2)}, u32[]{:S(2)}) %collective-permute-start.3) | collective-permute-done | bytes 98336 | tf_op jit(solution)/shard_map/ppermute | solution.py:750
  9.7 4.2 %collective-permute-start.5 = (f32[2,176,128]{2,1,0:T(8,128)S(1)}, f32[2,176,128]{2,1,0:T(8,128)S(1)}, u32[]{:S(2)}, u32[]{:S(2)}) collective-permute-start(f32[2,176,128]{2,1,0:T(8,128)S(1)} %get-tuple-element.50), channel_id=1, source_target_pairs={{0,2},{1,8},{2,0},{3,10},{4,6},{5,12},{6,4},{7,14},{8,1},{9,16},{1... | collective-permute-start | bytes 540680 | tf_op jit(solution)/shard_map/ppermute | solution.py:716
  13.8 1.4 %collective-permute-done.4.refs_4_ = f32[2,160,128]{2,1,0:T(8,128)S(1)} collective-permute-done((f32[2,160,128]{2,1,0:T(8,128)S(1)}, f32[2,160,128]{2,1,0:T(8,128)S(1)}, u32[]{:S(2)}, u32[]{:S(2)}) %collective-permute-start.4) | collective-permute-done | bytes 163872 | tf_op jit(solution)/shard_map/ppermute | solution.py:717
  15.2 2.1 %collective-permute-done.5.refs_5_ = f32[2,176,128]{2,1,0:T(8,128)S(1)} collective-permute-done((f32[2,176,128]{2,1,0:T(8,128)S(1)}, f32[2,176,128]{2,1,0:T(8,128)S(1)}, u32[]{:S(2)}, u32[]{:S(2)}) %collective-permute-start.5) | collective-permute-done | bytes 180256 | tf_op jit(solution)/shard_map/ppermute | solution.py:716
  17.3 1.5 %first.1 = (f32[5,2,6,32,128]{4,3,2,1,0:T(8,128)S(1)}, f32[18,2,4,16,128]{4,3,2,1,0:T(8,128)S(1)}, f32[6,2,4,16,128]{4,3,2,1,0:T(8,128)S(1)}, f32[19,2,4,16,128]...) custom-call(f32[33,4,16,128]{3,2,1,0:T(8,128)S(1)} %get-tuple-elemen, ...), custom_call_target="tpu_custom_call" | custom-call | flops 100000 | tf_op jit(solution)/shard_map/first/pallas_call | solution.py:722
  18.8 2.1 %collective-permute-start.7 = (f32[2,120,128]{2,1,0:T(8,128)S(1)}, f32[2,120,128]{2,1,0:T(8,128)S(1)}, u32[]{:S(2)}, u32[]{:S(2)}) collective-permute-start(f32[2,120,128]{2,1,0:T(8,128)S(1)} %get-tuple-element.57), channel_id=1, source_target_pairs={{0,2},{1,8},{2,0},{3,10},{4,6},{5,12},{6,4},{7,14},{8,1},{9,16},{1... | collective-permute-start | bytes 368648 | tf_op jit(solution)/shard_map/ppermute | solution.py:716
  20.9 2.9 %collective-permute-done.7.refs_2_.refs_6_ = f32[2,120,128]{2,1,0:T(8,128)S(1)} collective-permute-done((f32[2,120,128]{2,1,0:T(8,128)S(1)}, f32[2,120,128]{2,1,0:T(8,128)S(1)}, u32[]{:S(2)}, u32[]{:S(2)}) %collective-permute-start.7) | collective-permute-done | bytes 122912 | tf_op jit(solution)/shard_map/ppermute | solution.py:716
  23.9 2.1 %collective-permute-start.8 = (f32[2,40,128]{2,1,0:T(8,128)S(1)}, f32[2,40,128]{2,1,0:T(8,128)S(1)}, u32[]{:S(2)}, u32[]{:S(2)}) collective-permute-start(f32[2,40,128]{2,1,0:T(8,128)S(1)} %get-tuple-element.61), channel_id=1, source_target_pairs={{0,2},{1,3},{2,0},{3,1},{4,6},{5,7},{6,4},{7,5},{8,10},{9,11},{10,... | collective-permute-start | bytes 122888 | tf_op jit(solution)/shard_map/ppermute | solution.py:717
  25.9 2.0 %collective-permute-done.8.refs_7_ = f32[2,40,128]{2,1,0:T(8,128)S(1)} collective-permute-done((f32[2,40,128]{2,1,0:T(8,128)S(1)}, f32[2,40,128]{2,1,0:T(8,128)S(1)}, u32[]{:S(2)}, u32[]{:S(2)}) %collective-permute-start.8) | collective-permute-done | bytes 40992 | tf_op jit(solution)/shard_map/ppermute | solution.py:717
  27.9 1.3 %next_1.1 = (f32[19,2,4,16,128]{4,3,2,1,0:T(8,128)S(1)}, f32[2,6,32,128]{3,2,1,0:T(8,128)S(1)}, f32[2,120,128]{2,1,0:T(8,128)S(1)}, f32[2,120,128]{2,1,0:T(8,128...) custom-call(f32[5,2,6,32,128]{4,3,2,1,0:T(8,128)S(1)} %get-tuple-element.51.refs_0_.state, ...), custom_call_target="tpu_custom_call" | custom-call | flops 100000 | tf_op jit(solution)/shard_map/next_1/pallas_call | solution.py:722
  29.3 3.1 %collective-permute-start.11 = (f32[2,120,128]{2,1,0:T(8,128)S(1)}, f32[2,120,128]{2,1,0:T(8,128)S(1)}, u32[]{:S(2)}, u32[]{:S(2)}) collective-permute-start(f32[2,120,128]{2,1,0:T(8,128)S(1)} %get-tuple-element.66), channel_id=1, source_target_pairs={{0,2},{1,8},{2,0},{3,10},{4,6},{5,12},{6,4},{7,14},{8,1},{9,16},{1... | collective-permute-start | bytes 368648 | tf_op jit(solution)/shard_map/ppermute | solution.py:716
  32.4 2.9 %collective-permute-done.11.refs_2_.refs_6_ = f32[2,120,128]{2,1,0:T(8,128)S(1)} collective-permute-done((f32[2,120,128]{2,1,0:T(8,128)S(1)}, f32[2,120,128]{2,1,0:T(8,128)S(1)}, u32[]{:S(2)}, u32[]{:S(2)}) %collective-permute-start.11) | collective-permute-done | bytes 122912 | tf_op jit(solution)/shard_map/ppermute | solution.py:716
  35.3 2.1 %collective-permute-start.12 = (f32[2,40,128]{2,1,0:T(8,128)S(1)}, f32[2,40,128]{2,1,0:T(8,128)S(1)}, u32[]{:S(2)}, u32[]{:S(2)}) collective-permute-start(f32[2,40,128]{2,1,0:T(8,128)S(1)} %get-tuple-element.70), channel_id=1, source_target_pairs={{0,2},{1,3},{2,0},{3,1},{4,6},{5,7},{6,4},{7,5},{8,10},{9,11},{10,... | collective-permute-start | bytes 122888 | tf_op jit(solution)/shard_map/ppermute | solution.py:717
  37.4 2.0 %collective-permute-done.12.refs_7_ = f32[2,40,128]{2,1,0:T(8,128)S(1)} collective-permute-done((f32[2,40,128]{2,1,0:T(8,128)S(1)}, f32[2,40,128]{2,1,0:T(8,128)S(1)}, u32[]{:S(2)}, u32[]{:S(2)}) %collective-permute-start.12) | collective-permute-done | bytes 40992 | tf_op jit(solution)/shard_map/ppermute | solution.py:717
  39.4 1.5 %next_0.1 = (f32[19,4,16,128]{3,2,1,0:T(8,128)S(1)}, f32[19,4,16,128]{3,2,1,0:T(8,128)S(1)}, f32[2,6,32,128]{3,2,1,0:T(8,128)S(1)}, f32[2,24,128]{2,1,0:T(8,128)...) custom-call(f32[5,2,6,32,128]{4,3,2,1,0:T(8,128)S(1)} %get-tuple-element.51.refs_0_.state, ...), custom_call_target="tpu_custom_call" | custom-call | flops 100000 | tf_op jit(solution)/shard_map/next_0/pallas_call | solution.py:722
  41.4 3.0 %collective-permute-start.16 = (f32[2,24,128]{2,1,0:T(8,128)S(1)}, f32[2,24,128]{2,1,0:T(8,128)S(1)}, u32[]{:S(2)}, u32[]{:S(2)}) collective-permute-start(f32[2,24,128]{2,1,0:T(8,128)S(1)} %get-tuple-element.77), channel_id=1, source_target_pairs={{0,2},{1,8},{2,0},{3,10},{4,6},{5,12},{6,4},{7,14},{8,1},{9,16},{1... | collective-permute-start | bytes 73736 | tf_op jit(solution)/shard_map/ppermute | solution.py:716
  44.4 1.8 %collective-permute-done.16.refs_2_ = f32[2,24,128]{2,1,0:T(8,128)S(1)} collective-permute-done((f32[2,24,128]{2,1,0:T(8,128)S(1)}, f32[2,24,128]{2,1,0:T(8,128)S(1)}, u32[]{:S(2)}, u32[]{:S(2)}) %collective-permute-start.16) | collective-permute-done | bytes 24608 | tf_op jit(solution)/shard_map/ppermute | solution.py:716
  46.3 2.1 %collective-permute-start.17 = (f32[2,8,128]{2,1,0:T(8,128)S(1)}, f32[2,8,128]{2,1,0:T(8,128)S(1)}, u32[]{:S(2)}, u32[]{:S(2)}) collective-permute-start(f32[2,8,128]{2,1,0:T(8,128)S(1)} %get-tuple-element.79), channel_id=1, source_target_pairs={{0,2},{1,3},{2,0},{3,1},{4,6},{5,7},{6,4},{7,5},{8,10},{9,11},{10,... | collective-permute-start | bytes 24584 | tf_op jit(solution)/shard_map/ppermute | solution.py:717
  48.3 1.7 %collective-permute-done.17.yr_a = f32[2,8,128]{2,1,0:T(8,128)S(1)} collective-permute-done((f32[2,8,128]{2,1,0:T(8,128)S(1)}, f32[2,8,128]{2,1,0:T(8,128)S(1)}, u32[]{:S(2)}, u32[]{:S(2)}) %collective-permute-start.17) | collective-permute-done | bytes 8224 | tf_op jit(solution)/shard_map/ppermute | solution.py:717
  50.2 1.2 %collective-permute-done.19.refs_3_ = f32[2,4,16,128]{3,2,1,0:T(8,128)S(1)} collective-permute-done((f32[2,4,16,128]{3,2,1,0:T(8,128)S(1)}, f32[2,4,16,128]{3,2,1,0:T(8,128)S(1)}, u32[]{:S(2)}, u32[]{:S(2)}) %collective-permute-start.19) | collective-permute-done | bytes 65568 | tf_op jit(solution)/shard_map/ppermute | solution.py:750
  51.4 1.1 %join.1 = (f32[19,8,16,128]{3,2,1,0:T(8,128)}, f32[8,16,128]{2,1,0:T(8,128)}) custom-call(f32[19,4,16,128]{3,2,1,0:T(8,128)S(1)} %get-tuple-element.73.refs_0_, f32[19,4,16,128]{3,2,1,0:T(8,128)S(1)} %collective-permute-done.14.refs_1_, f32[2,4,16,128]{3,2,1,0:T(8,128)S(1)} %get-tuple-element.82.refs_2_, f32[2,4,16,128]{3,2,1,0:T(8,128)S(1)} %collective-permute-done.19.refs_3_), custom_call_target="tpu_custom_call" | custom-call | flops 1000 | tf_op jit(solution)/shard_map/join/pallas_call | solution.py:722
  (27 shorter events, 1.9 us)
Async XLA Ops:
  2.4 7.2 %collective-permute-start = (f32[33,4,16,128]{3,2,1,0:T(8,128)S(1)}, f32[33,4,16,128]{3,2,1,0:T(8,128)S(1)}, u32[]{:S(2)}, u32[]{:S(2)}) collective-permute-start(f32[33,4,16,128]{3,2,1,0:T(8,128)S(1)} %get-tuple-element.44), channel_id=1, source_target_pairs={{0,1},{1,0},{2,3},{3,2},{4,5},{5,4},{6,7},{7,6},{8,9},{9,8},{10,11... | collective-permute-start | bytes 3244040 | tf_op jit(solution)/shard_map/ppermute | solution.py:750
  2.9 5.2 %collective-permute-start.1 = (f32[8,16,128]{2,1,0:T(8,128)S(1)}, f32[8,16,128]{2,1,0:T(8,128)S(1)}, u32[]{:S(2)}, u32[]{:S(2)}) collective-permute-start(f32[8,16,128]{2,1,0:T(8,128)S(1)} %get-tuple-element.45), channel_id=1, source_target_pairs={{0,2},{1,3},{2,0},{3,1},{4,6},{5,7},{6,4},{7,5},{8,10},{9,11},{10,... | collective-permute-start | bytes 196616 | tf_op jit(solution)/shard_map/ppermute | solution.py:717
  5.5 2.7 %collective-permute-start.2 = (f32[8,16,128]{2,1,0:T(8,128)S(1)}, f32[8,16,128]{2,1,0:T(8,128)S(1)}, u32[]{:S(2)}, u32[]{:S(2)}) collective-permute-start(f32[8,16,128]{2,1,0:T(8,128)S(1)} %get-tuple-element.46), channel_id=1, source_target_pairs={{0,1},{1,0},{2,4},{3,5},{4,2},{5,3},{6,7},{7,6},{8,9},{9,8},{10,12... | collective-permute-start | bytes 196616 | tf_op jit(solution)/shard_map/ppermute | solution.py:716
  8.2 1.4 %collective-permute-start.3 = (f32[6,32,128]{2,1,0:T(8,128)S(1)}, f32[6,32,128]{2,1,0:T(8,128)S(1)}, u32[]{:S(2)}, u32[]{:S(2)}) collective-permute-start(f32[6,32,128]{2,1,0:T(8,128)S(1)} %get-tuple-element.48), channel_id=1, source_target_pairs={{0,1},{1,0},{2,3},{3,2},{4,5},{5,4},{6,7},{7,6},{8,9},{9,8},{10,11... | collective-permute-start | bytes 294920 | tf_op jit(solution)/shard_map/ppermute | solution.py:750
  9.7 7.6 %collective-permute-start.5 = (f32[2,176,128]{2,1,0:T(8,128)S(1)}, f32[2,176,128]{2,1,0:T(8,128)S(1)}, u32[]{:S(2)}, u32[]{:S(2)}) collective-permute-start(f32[2,176,128]{2,1,0:T(8,128)S(1)} %get-tuple-element.50), channel_id=1, source_target_pairs={{0,2},{1,8},{2,0},{3,10},{4,6},{5,12},{6,4},{7,14},{8,1},{9,16},{1... | collective-permute-start | bytes 540680 | tf_op jit(solution)/shard_map/ppermute | solution.py:716
  13.8 1.4 %collective-permute-start.4 = (f32[2,160,128]{2,1,0:T(8,128)S(1)}, f32[2,160,128]{2,1,0:T(8,128)S(1)}, u32[]{:S(2)}, u32[]{:S(2)}) collective-permute-start(f32[2,160,128]{2,1,0:T(8,128)S(1)} %get-tuple-element.49), channel_id=1, source_target_pairs={{0,1},{1,0},{2,3},{3,2},{4,5},{5,4},{6,7},{7,6},{8,9},{9,8},{10,11... | collective-permute-start | bytes 491528 | tf_op jit(solution)/shard_map/ppermute | solution.py:717
  18.8 2.2 %collective-permute-start.6 = (f32[2,120,128]{2,1,0:T(8,128)S(1)}, f32[2,120,128]{2,1,0:T(8,128)S(1)}, u32[]{:S(2)}, u32[]{:S(2)}) collective-permute-start(f32[2,120,128]{2,1,0:T(8,128)S(1)} %get-tuple-element.56), channel_id=1, source_target_pairs={{0,1},{1,0},{2,3},{3,2},{4,5},{5,4},{6,7},{7,6},{8,9},{9,8},{10,11... | collective-permute-start | bytes 368648 | tf_op jit(solution)/shard_map/ppermute | solution.py:717
  18.8 4.9 %collective-permute-start.7 = (f32[2,120,128]{2,1,0:T(8,128)S(1)}, f32[2,120,128]{2,1,0:T(8,128)S(1)}, u32[]{:S(2)}, u32[]{:S(2)}) collective-permute-start(f32[2,120,128]{2,1,0:T(8,128)S(1)} %get-tuple-element.57), channel_id=1, source_target_pairs={{0,2},{1,8},{2,0},{3,10},{4,6},{5,12},{6,4},{7,14},{8,1},{9,16},{1... | collective-permute-start | bytes 368648 | tf_op jit(solution)/shard_map/ppermute | solution.py:716
  23.9 4.1 %collective-permute-start.8 = (f32[2,40,128]{2,1,0:T(8,128)S(1)}, f32[2,40,128]{2,1,0:T(8,128)S(1)}, u32[]{:S(2)}, u32[]{:S(2)}) collective-permute-start(f32[2,40,128]{2,1,0:T(8,128)S(1)} %get-tuple-element.61), channel_id=1, source_target_pairs={{0,2},{1,3},{2,0},{3,1},{4,6},{5,7},{6,4},{7,5},{8,10},{9,11},{10,... | collective-permute-start | bytes 122888 | tf_op jit(solution)/shard_map/ppermute | solution.py:717
  25.9 2.0 %collective-permute-start.9 = (f32[2,40,128]{2,1,0:T(8,128)S(1)}, f32[2,40,128]{2,1,0:T(8,128)S(1)}, u32[]{:S(2)}, u32[]{:S(2)}) collective-permute-start(f32[2,40,128]{2,1,0:T(8,128)S(1)} %get-tuple-element.62), channel_id=1, source_target_pairs={{0,1},{1,0},{2,4},{3,5},{4,2},{5,3},{6,7},{7,6},{8,9},{9,8},{10,12... | collective-permute-start | bytes 122888 | tf_op jit(solution)/shard_map/ppermute | solution.py:716
  29.2 3.1 %collective-permute-start.10 = (f32[2,120,128]{2,1,0:T(8,128)S(1)}, f32[2,120,128]{2,1,0:T(8,128)S(1)}, u32[]{:S(2)}, u32[]{:S(2)}) collective-permute-start(f32[2,120,128]{2,1,0:T(8,128)S(1)} %get-tuple-element.65), channel_id=1, source_target_pairs={{0,1},{1,0},{2,3},{3,2},{4,5},{5,4},{6,7},{7,6},{8,9},{9,8},{10,11... | collective-permute-start | bytes 368648 | tf_op jit(solution)/shard_map/ppermute | solution.py:717
  29.3 5.9 %collective-permute-start.11 = (f32[2,120,128]{2,1,0:T(8,128)S(1)}, f32[2,120,128]{2,1,0:T(8,128)S(1)}, u32[]{:S(2)}, u32[]{:S(2)}) collective-permute-start(f32[2,120,128]{2,1,0:T(8,128)S(1)} %get-tuple-element.66), channel_id=1, source_target_pairs={{0,2},{1,8},{2,0},{3,10},{4,6},{5,12},{6,4},{7,14},{8,1},{9,16},{1... | collective-permute-start | bytes 368648 | tf_op jit(solution)/shard_map/ppermute | solution.py:716
  35.3 4.1 %collective-permute-start.12 = (f32[2,40,128]{2,1,0:T(8,128)S(1)}, f32[2,40,128]{2,1,0:T(8,128)S(1)}, u32[]{:S(2)}, u32[]{:S(2)}) collective-permute-start(f32[2,40,128]{2,1,0:T(8,128)S(1)} %get-tuple-element.70), channel_id=1, source_target_pairs={{0,2},{1,3},{2,0},{3,1},{4,6},{5,7},{6,4},{7,5},{8,10},{9,11},{10,... | collective-permute-start | bytes 122888 | tf_op jit(solution)/shard_map/ppermute | solution.py:717
  37.4 2.0 %collective-permute-start.13 = (f32[2,40,128]{2,1,0:T(8,128)S(1)}, f32[2,40,128]{2,1,0:T(8,128)S(1)}, u32[]{:S(2)}, u32[]{:S(2)}) collective-permute-start(f32[2,40,128]{2,1,0:T(8,128)S(1)} %get-tuple-element.71), channel_id=1, source_target_pairs={{0,1},{1,0},{2,4},{3,5},{4,2},{5,3},{6,7},{7,6},{8,9},{9,8},{10,12... | collective-permute-start | bytes 122888 | tf_op jit(solution)/shard_map/ppermute | solution.py:716
  40.8 10.6 %collective-permute-start.14 = (f32[19,4,16,128]{3,2,1,0:T(8,128)S(1)}, f32[19,4,16,128]{3,2,1,0:T(8,128)S(1)}, u32[]{:S(2)}, u32[]{:S(2)}) collective-permute-start(f32[19,4,16,128]{3,2,1,0:T(8,128)S(1)} %get-tuple-element.74), channel_id=1, source_target_pairs={{0,1},{1,0},{2,3},{3,2},{4,5},{5,4},{6,7},{7,6},{8,9},{9,8},{10,11... | collective-permute-start | bytes 1867784 | tf_op jit(solution)/shard_map/ppermute | solution.py:750
  40.9 3.5 %collective-permute-start.15 = (f32[2,24,128]{2,1,0:T(8,128)S(1)}, f32[2,24,128]{2,1,0:T(8,128)S(1)}, u32[]{:S(2)}, u32[]{:S(2)}) collective-permute-start(f32[2,24,128]{2,1,0:T(8,128)S(1)} %get-tuple-element.76), channel_id=1, source_target_pairs={{0,1},{1,0},{2,3},{3,2},{4,5},{5,4},{6,7},{7,6},{8,9},{9,8},{10,11... | collective-permute-start | bytes 73736 | tf_op jit(solution)/shard_map/ppermute | solution.py:717
  41.4 4.8 %collective-permute-start.16 = (f32[2,24,128]{2,1,0:T(8,128)S(1)}, f32[2,24,128]{2,1,0:T(8,128)S(1)}, u32[]{:S(2)}, u32[]{:S(2)}) collective-permute-start(f32[2,24,128]{2,1,0:T(8,128)S(1)} %get-tuple-element.77), channel_id=1, source_target_pairs={{0,2},{1,8},{2,0},{3,10},{4,6},{5,12},{6,4},{7,14},{8,1},{9,16},{1... | collective-permute-start | bytes 73736 | tf_op jit(solution)/shard_map/ppermute | solution.py:716
  46.3 3.8 %collective-permute-start.17 = (f32[2,8,128]{2,1,0:T(8,128)S(1)}, f32[2,8,128]{2,1,0:T(8,128)S(1)}, u32[]{:S(2)}, u32[]{:S(2)}) collective-permute-start(f32[2,8,128]{2,1,0:T(8,128)S(1)} %get-tuple-element.79), channel_id=1, source_target_pairs={{0,2},{1,3},{2,0},{3,1},{4,6},{5,7},{6,4},{7,5},{8,10},{9,11},{10,... | collective-permute-start | bytes 24584 | tf_op jit(solution)/shard_map/ppermute | solution.py:717
  48.3 1.7 %collective-permute-start.18 = (f32[2,8,128]{2,1,0:T(8,128)S(1)}, f32[2,8,128]{2,1,0:T(8,128)S(1)}, u32[]{:S(2)}, u32[]{:S(2)}) collective-permute-start(f32[2,8,128]{2,1,0:T(8,128)S(1)} %get-tuple-element.80), channel_id=1, source_target_pairs={{0,1},{1,0},{2,4},{3,5},{4,2},{5,3},{6,7},{7,6},{8,9},{9,8},{10,12... | collective-permute-start | bytes 24584 | tf_op jit(solution)/shard_map/ppermute | solution.py:716
  50.1 1.3 %collective-permute-start.19 = (f32[2,4,16,128]{3,2,1,0:T(8,128)S(1)}, f32[2,4,16,128]{3,2,1,0:T(8,128)S(1)}, u32[]{:S(2)}, u32[]{:S(2)}) collective-permute-start(f32[2,4,16,128]{3,2,1,0:T(8,128)S(1)} %get-tuple-element.83), channel_id=1, source_target_pairs={{0,1},{1,0},{2,3},{3,2},{4,5},{5,4},{6,7},{7,6},{8,9},{9,8},{10,11... | collective-permute-start | bytes 196616 | tf_op jit(solution)/shard_map/ppermute | solution.py:750
